TPU v7x, 32 devices: a whole 2x2x4 slice. The times are simulated.
32 devices in a mesh: groups: 2 (over x), pb: 16 (over z, y, core).
Axes of the slice: x: 2, y: 2, z: 4, core: 2. Of those that a mesh axis runs over, the one named last changes fastest.
Arguments:
- tokens: bfloat16 [6144, 512], P(('groups', 'pb')), parts along dimension 0, may hold values from -6 to 6
- stamps: int32 [6144], P(('groups', 'pb')), parts along dimension 0, may hold values from 0 to 1086324736, as said below
- norm_gain: float32 [512], replicated, may hold values from 0.5 to 1.5
- w_proj: bfloat16 [512, 2048], replicated, may hold values from -0.25 to 0.25
- rel_bias: float32 [8, 16], replicated, may hold values from -1.5 to 1.5
- attn_gain: float32 [512], replicated, may hold values from 0.5 to 1.5
- w_out: bfloat16 [512, 512], replicated, may hold values from -0.25 to 0.25
Outputs:
- mixed: bfloat16 [6144, 512], P(('groups', 'pb')), parts along dimension 0
There are 2 independent parts, one for each index of `groups`. A program takes and returns all parts, laid end to end along the dimension named above; an argument that names none is the same for every part. Nothing has to cross between parts.
Inputs may be any that keep to these rules, and one draw needn't show every extreme that they name: `stamps`: stamps never fall from one row to the next.
All inputs are finite; a program needn't handle non-finite values.
Results may differ from a plain program's by a relative error of at most 0.008.
Values may be sent and summed in bfloat16 or wider, within the bound.
A program may use at most 128 MiB of HBM per device.

v0:
```python
import functools

import jax
import jax.numpy as jnp
from jax import lax
from jax.experimental import pallas as pl
from jax.experimental.pallas import tpu as pltpu
from jax.sharding import PartitionSpec as P

EPSILON = 1e-05
LANES = 128


def layer_norm(values, gain):
    centered = values - jnp.mean(values, axis=-1, keepdims=True)
    spread = jnp.mean(centered * centered, axis=-1, keepdims=True)
    return centered * lax.rsqrt(spread + EPSILON) * gain


def kernel(
    parts,
    heads,
    tokens_hbm,
    stamps_hbm,
    norm_gain_hbm,
    w_proj_hbm,
    bias_hbm,
    attn_gain_hbm,
    w_out_hbm,
    out_ref,
    tokens_ref,
    stamps_ref,
    norm_gain_ref,
    w_proj_ref,
    bias_ref,
    attn_gain_ref,
    w_out_ref,
    kv_send,
    q_send,
    kv_all,
    q_all,
    query_buf,
    stamp_all,
    stamp_keys,
    stamp_rows,
    total_buf,
    gate_buf,
    back_buf,
    att_buf,
    load_sem,
    kv_send_sem,
    q_send_sem,
    fwd_sem,
    kv_sem,
    q_sem,
    stamp_send_sem,
    stamp_sem,
    back_sem,
    att_sem,
):
    rows, width = tokens_ref.shape
    half = rows // 2
    head_size = width // heads
    splits = parts // heads
    slots = heads
    near = slots // 2
    blocks_per_tile = max(1, 384 // rows)
    key_tile = blocks_per_tile * rows
    group_tiles = splits // blocks_per_tile
    buckets = bias_ref.shape[1]

    loads = [
        pltpu.make_async_copy(source, target, load_sem.at[index])
        for index, (source, target) in enumerate(
            [
                (tokens_hbm, tokens_ref),
                (norm_gain_hbm, norm_gain_ref),
                (w_proj_hbm.at[:, width:], w_proj_ref.at[:, width:]),
                (stamps_hbm, stamps_ref),
                (bias_hbm, bias_ref),
                (w_proj_hbm.at[:, :width], w_proj_ref.at[:, :width]),
                (attn_gain_hbm, attn_gain_ref),
                (w_out_hbm, w_out_ref),
            ]
        )
    ]
    for load in loads:
        load.start()

    me = lax.axis_index("pb")
    my_head = me // splits
    my_split = me % splits
    upper = my_head // near
    my_place = my_head % near
    near_first = upper * near
    far_first = near - near_first

    def split_of(block):
        place = block % splits
        odd = (block // splits) % 2
        return place + odd * (splits - 1 - 2 * place)

    def block_of(slot, split):
        odd = slot % 2
        return slot * splits + split + odd * (splits - 1 - 2 * split)

    def remote(source, target, send, receive, device):
        return pltpu.make_async_remote_copy(
            src_ref=source,
            dst_ref=target,
            send_sem=send,
            recv_sem=receive,
            device_id={"pb": device},
            device_id_type=pl.DeviceIdType.MESH,
        )

    barrier = pltpu.get_barrier_semaphore()

    def greet(step, carry):
        other = lax.rem(me + step, parts)
        pl.semaphore_signal(
            barrier, inc=1, device_id={"pb": other}, device_id_type=pl.DeviceIdType.MESH
        )
        return carry

    lax.fori_loop(1, parts, greet, 0)

    low = lax.broadcasted_iota(jnp.int32, (1, LANES), 1) < head_size

    for load in loads[:3]:
        load.wait()
    normed = layer_norm(tokens_ref[...].astype(jnp.float32), norm_gain_ref[...]).astype(jnp.bfloat16)
    front = jnp.dot(normed, w_proj_ref[:, width : 2 * width], preferred_element_type=jnp.float32)
    scaled = front.astype(jnp.bfloat16).astype(jnp.float32) * (0.5 * head_size ** (-0.5))
    back = jnp.dot(normed, w_proj_ref[:, 2 * width :], preferred_element_type=jnp.float32)
    for pair in range(heads // 2):
        cols = slice(pair * LANES, (pair + 1) * LANES)
        key_cols = back[:, :width][:, cols]
        value_cols = back[:, width:][:, cols]
        query_cols = scaled[:, cols]
        kv_send[2 * pair] = jnp.where(
            low, key_cols, pltpu.roll(value_cols, head_size, 1)
        ).astype(jnp.bfloat16)
        kv_send[2 * pair + 1] = jnp.where(
            low, pltpu.roll(key_cols, head_size, 1), value_cols
        ).astype(jnp.bfloat16)
        top, bottom = query_cols[:half], query_cols[half:]
        q_send[2 * pair] = jnp.where(low, top, pltpu.roll(bottom, head_size, 1)).astype(jnp.bfloat16)
        q_send[2 * pair + 1] = jnp.where(low, pltpu.roll(top, head_size, 1), bottom).astype(jnp.bfloat16)
    loads[3].wait()
    loads[4].wait()

    my_home = split_of(me)

    def stamp_copy(target):
        return remote(
            stamps_ref, stamp_all.at[me], stamp_send_sem.at[target], stamp_sem.at[me], target
        )

    def kv_copy(head, target):
        return remote(kv_send.at[head], kv_all.at[me], kv_send_sem.at[head], kv_sem.at[me], target)

    def q_copy(head, target):
        return remote(q_send.at[head], q_all.at[my_head], q_send_sem.at[head], q_sem.at[my_head], target)

    def each_head(first, act):
        def one(step, carry):
            head = first + lax.rem(my_place + step, near)
            target = head * splits + my_home

            @pl.when(target != me)
            def _():
                act(head, target)

            return carry

        lax.fori_loop(0, near, one, 0)

    def send_stamps(step, carry):
        stamp_copy(lax.rem(me + step, parts)).start()
        return carry

    def start_both(head, target):
        q_copy(head, target).start()
        kv_copy(head, target).start()

    pl.semaphore_wait(barrier, parts - 1)
    lax.fori_loop(1, parts, send_stamps, 0)
    each_head(near_first, start_both)
    each_head(far_first, lambda head, target: q_copy(head, target).start())
    each_head(far_first, lambda head, target: kv_copy(head, target).start())

    stamp_all[me] = stamps_ref[...]

    @pl.when(my_home == my_split)
    def _():
        kv_all[me] = kv_send[my_head]
        q_all[my_head] = q_send[my_head]

    loads[5].wait()
    gate_proj = jnp.dot(normed, w_proj_ref[:, :width], preferred_element_type=jnp.float32)
    gate_buf[...] = jax.nn.silu(gate_proj).astype(jnp.bfloat16)
    total_buf[...] = jnp.zeros_like(total_buf)

    zeros_count = lax.broadcasted_iota(jnp.int32, (8, LANES), 1)
    bucket = jnp.clip((33 - zeros_count) >> 1, 0, buckets - 1)
    table = jnp.zeros((8, LANES), jnp.float32)
    for bucket_id in range(buckets):
        table = jnp.where(bucket == bucket_id, 0.5 * bias_ref[my_head, bucket_id], table)
    table_two = jnp.broadcast_to(table[:1], (2 * rows, LANES))
    table = table_two[:rows]

    def wait_stamps(step, carry):
        source = lax.rem(me + step, parts)
        remote(
            stamps_ref, stamp_all.at[source], stamp_send_sem.at[source], stamp_sem.at[source], source
        ).wait_recv()
        return carry

    lax.fori_loop(1, parts, wait_stamps, 0)

    for tile in range(parts // blocks_per_tile):
        stamp_keys[tile] = jnp.concatenate(
            [stamp_all[tile * blocks_per_tile + place] for place in range(blocks_per_tile)], axis=1
        )

    def turn_stamps(slot, carry):
        block = block_of(slot, my_split)
        stamp_rows[slot] = jnp.transpose(jnp.broadcast_to(stamp_all[block], (LANES, rows)))
        return carry

    lax.fori_loop(0, slots, turn_stamps, 0)

    def forward(slot, source, step):
        peer = my_head * splits + lax.rem(my_split + step, splits)
        return remote(
            kv_all.at[source], kv_all.at[source], fwd_sem.at[slot, step], kv_sem.at[source], peer
        )

    def take_direct(slot):
        source = block_of(slot, my_split)

        @pl.when(source != me)
        def _():
            remote(
                kv_send.at[0], kv_all.at[source], kv_send_sem.at[0], kv_sem.at[source], source
            ).wait_recv()

        for step in range(1, splits):
            forward(slot, source, step).start()

    def take_forwarded(slot):
        for step in range(1, splits):
            source = block_of(slot, lax.rem(my_split + step, splits))
            forward(slot, source, step).wait_recv()

    def take_query(slot):
        source = block_of(slot, my_split)

        @pl.when(source != me)
        def _():
            remote(
                q_send.at[0], q_all.at[slot], q_send_sem.at[0], q_sem.at[slot], source
            ).wait_recv()

        packed = q_all[slot].astype(jnp.float32)
        query_buf[slot] = jnp.concatenate(
            [jnp.where(low, packed, 0.0), jnp.where(low, pltpu.roll(packed, head_size, 1), 0.0)], axis=0
        ).astype(jnp.bfloat16)

    row_id = lax.broadcasted_iota(jnp.int32, (rows, LANES), 0)
    col_id = lax.broadcasted_iota(jnp.int32, (rows, LANES), 1)

    def visit_tile(slot, block, tile, masked):
        key_value = kv_all[pl.ds(tile * blocks_per_tile, blocks_per_tile)]
        key_value = key_value.reshape(key_tile, LANES)
        scores = lax.dot_general(
            query_buf[slot], key_value, (((1,), (1,)), ((), ())), preferred_element_type=jnp.float32
        )
        query_stamp = stamp_rows[slot]
        weights = []
        for first in range(0, key_tile, LANES):
            elapsed = query_stamp - stamp_keys[tile, :, first : first + LANES]
            bias = jnp.take_along_axis(table, lax.clz(elapsed), axis=1, mode="promise_in_bounds")
            halved = scores[:, first : first + LANES] + bias
            weight = halved + halved * jnp.tanh(halved)
            if masked:
                ahead = tile * key_tile + first - block * rows
                weight = jnp.where(col_id + ahead <= row_id, weight, 0.0)
            weights.append(weight.astype(jnp.bfloat16))
        total_buf[slot] += jnp.dot(
            jnp.concatenate(weights, axis=1), key_value, preferred_element_type=jnp.float32
        )

    def visit_two(slot, group):
        def one(tile, carry):
            key_value = kv_all[pl.ds(tile * blocks_per_tile, blocks_per_tile)]
            key_value = key_value.reshape(key_tile, LANES)
            queries = query_buf[pl.ds(slot, 2)].reshape(2 * rows, LANES)
            query_stamp = stamp_rows[pl.ds(slot, 2)].reshape(2 * rows, LANES)
            scores = lax.dot_general(
                queries, key_value, (((1,), (1,)), ((), ())), preferred_element_type=jnp.float32
            )
            weights = []
            for first in range(0, key_tile, LANES):
                elapsed = query_stamp - stamp_keys[tile, :, first : first + LANES]
                bias = jnp.take_along_axis(table_two, lax.clz(elapsed), axis=1, mode="promise_in_bounds")
                halved = scores[:, first : first + LANES] + bias
                weights.append((halved + halved * jnp.tanh(halved)).astype(jnp.bfloat16))
            sums = jnp.dot(
                jnp.concatenate(weights, axis=1), key_value, preferred_element_type=jnp.float32
            )
            total_buf[pl.ds(slot, 2)] += sums.reshape(2, rows, LANES)
            return carry

        lax.fori_loop(group * group_tiles, (group + 1) * group_tiles, one, 0)

    def visit_later(first, end, group):
        count = end - first

        def two(step, carry):
            visit_two(first + 2 * step, group)
            return carry

        lax.fori_loop(0, count // 2, two, 0)

        @pl.when(count % 2 == 1)
        def _():
            visit_before(end - 1, group)

    def visit_before(slot, group):
        def one(tile, carry):
            visit_tile(slot, 0, tile, False)
            return carry

        lax.fori_loop(group * group_tiles, (group + 1) * group_tiles, one, 0)

    def visit_own(slot):
        block = block_of(slot, my_split)
        last = block // blocks_per_tile

        def one(tile, carry):
            visit_tile(slot, block, tile, False)
            return carry

        if group_tiles > 1:
            lax.fori_loop(slot * group_tiles, last, one, 0)
        visit_tile(slot, block, last, True)

    def send_back(slot, target):
        return remote(
            back_buf.at[slot], att_buf.at[my_head], back_sem.at[slot], att_sem.at[my_head], target
        )

    def finish(slot, carry):
        block = block_of(slot, my_split)
        total = total_buf[slot]
        result = jnp.where(low, pltpu.roll(total[:half], head_size, 1), total[half:]).astype(jnp.bfloat16)
        back_buf[slot] = result

        @pl.when(block == me)
        def _():
            att_buf[my_head] = result

        @pl.when(block != me)
        def _():
            send_back(slot, block).start()

        return carry

    def take_near(slot, carry):
        take_direct(slot)
        take_query(slot)
        return carry

    lax.fori_loop(near_first, near_first + near, take_near, 0)

    def near_group(group, carry):
        take_forwarded(group)
        visit_own(group)

        visit_later(group + 1, near_first + near, group)
        return carry

    lax.fori_loop(near_first, near_first + near, near_group, 0)

    lower_end = near * (1 - upper)
    lax.fori_loop(0, lower_end, finish, 0)

    def far_query(slot, carry):
        take_query(slot)
        return carry

    lax.fori_loop(far_first, far_first + near, far_query, 0)

    def later_queries(group, carry):
        visit_later(near, slots, group)
        return carry

    lax.fori_loop(0, lower_end, later_queries, 0)

    def far_at(step):
        return far_first + lax.rem(my_place - step + near, near)

    take_direct(far_at(0))

    def far_group(step, carry):
        group = far_at(step)
        take_forwarded(group)

        @pl.when(step + 1 < near)
        def _():
            take_direct(far_at(step + 1))

        visit_own(group)
        visit_later(group + 1, slots, group)
        return carry

    lax.fori_loop(0, near - 1, far_group, 0)

    last_group = far_at(near - 1)
    lax.fori_loop(lower_end, last_group, finish, 0)
    take_forwarded(last_group)
    visit_own(last_group)
    finish(last_group, 0)

    def last_one(slot, carry):
        visit_before(slot, last_group)
        return finish(slot, carry)

    lax.fori_loop(last_group + 1, slots, last_one, 0)

    def drain_both(head, target):
        q_copy(head, target).wait_send()
        kv_copy(head, target).wait_send()

    each_head(near_first, drain_both)
    each_head(far_first, drain_both)

    def drain(step, carry):
        stamp_copy(lax.rem(me + step, parts)).wait_send()
        return carry

    lax.fori_loop(1, parts, drain, 0)

    def drain_slot(slot, carry):
        source = block_of(slot, my_split)
        for step in range(1, splits):
            forward(slot, source, step).wait_send()

        @pl.when(source != me)
        def _():
            send_back(slot, source).wait_send()

        return carry

    lax.fori_loop(0, slots, drain_slot, 0)
    loads[6].wait()
    loads[7].wait()

    def take_back(step, carry):
        head = lax.rem(my_head + step, heads)
        source = head * splits + my_home

        @pl.when(source != me)
        def _():
            remote(
                back_buf.at[0], att_buf.at[head], back_sem.at[0], att_sem.at[head], source
            ).wait_recv()

        return carry

    lax.fori_loop(0, heads, take_back, 0)

    pieces = []
    for pair in range(heads // 2):
        even = att_buf[2 * pair].astype(jnp.float32)
        odd = att_buf[2 * pair + 1].astype(jnp.float32)
        pieces.append(
            jnp.concatenate(
                [
                    jnp.where(low, even, pltpu.roll(odd, head_size, 1)),
                    jnp.where(low, pltpu.roll(even, head_size, 1), odd),
                ],
                axis=0,
            )
        )
    attended = jnp.concatenate(pieces, axis=1)
    gated = layer_norm(attended, attn_gain_ref[...]) * gate_buf[...].astype(jnp.float32)
    mixed = tokens_ref[...].astype(jnp.float32) + jnp.dot(
        gated.astype(jnp.bfloat16), w_out_ref[...], preferred_element_type=jnp.float32
    )
    out_ref[...] = mixed.astype(jnp.bfloat16)


def solution(mesh):
    parts = mesh.shape["pb"]

    def body(tokens, stamps, norm_gain, w_proj, rel_bias, attn_gain, w_out):
        rows, width = tokens.shape
        heads = rel_bias.shape[0]
        splits = parts // heads
        slots = parts // splits
        blocks_per_tile = max(1, 384 // rows)
        vmem = pl.BlockSpec(memory_space=pltpu.VMEM)
        return pl.pallas_call(
            functools.partial(kernel, parts, heads),
            out_shape=jax.ShapeDtypeStruct((rows, width), jnp.bfloat16),
            in_specs=[pl.BlockSpec(memory_space=pltpu.HBM)] * 7,
            out_specs=vmem,
            scratch_shapes=[
                pltpu.VMEM((rows, width), jnp.bfloat16),
                pltpu.VMEM((1, rows), jnp.int32),
                pltpu.VMEM((1, width), jnp.float32),
                pltpu.VMEM(w_proj.shape, jnp.bfloat16),
                pltpu.SMEM(rel_bias.shape, jnp.float32),
                pltpu.VMEM((1, width), jnp.float32),
                pltpu.VMEM(w_out.shape, jnp.bfloat16),
                pltpu.VMEM((heads, rows, LANES), jnp.bfloat16),
                pltpu.VMEM((heads, rows // 2, LANES), jnp.bfloat16),
                pltpu.VMEM((parts, rows, LANES), jnp.bfloat16),
                pltpu.VMEM((slots, rows // 2, LANES), jnp.bfloat16),
                pltpu.VMEM((slots, rows, LANES), jnp.bfloat16),
                pltpu.VMEM((parts, 1, rows), jnp.int32),
                pltpu.VMEM((parts // blocks_per_tile, 1, blocks_per_tile * rows), jnp.int32),
                pltpu.VMEM((slots, rows, LANES), jnp.int32),
                pltpu.VMEM((slots, rows, LANES), jnp.float32),
                pltpu.VMEM((rows, width), jnp.bfloat16),
                pltpu.VMEM((slots, rows // 2, LANES), jnp.bfloat16),
                pltpu.VMEM((heads, rows // 2, LANES), jnp.bfloat16),
                pltpu.SemaphoreType.DMA((8,)),
                pltpu.SemaphoreType.DMA((heads,)),
                pltpu.SemaphoreType.DMA((heads,)),
                pltpu.SemaphoreType.DMA((slots, splits)),
                pltpu.SemaphoreType.DMA((parts,)),
                pltpu.SemaphoreType.DMA((slots,)),
                pltpu.SemaphoreType.DMA((parts,)),
                pltpu.SemaphoreType.DMA((parts,)),
                pltpu.SemaphoreType.DMA((slots,)),
                pltpu.SemaphoreType.DMA((heads,)),
            ],
            compiler_params=pltpu.CompilerParams(
                collective_id=0, has_side_effects=True
            ),
        )(
            tokens,
            stamps.reshape(1, rows),
            norm_gain.reshape(1, width),
            w_proj,
            rel_bias,
            attn_gain.reshape(1, width),
            w_out,
        )

    return jax.shard_map(
        body,
        mesh=mesh,
        in_specs=(P(("groups", "pb"), None), P(("groups", "pb")), P(), P(), P(), P(), P()),
        out_specs=P(("groups", "pb"), None),
        check_vma=False,
    )
```

profile of v0, /device:TPU:0, one launch (start us, length us, event | category | flops | bytes accessed | tf_op | source)
XLA Modules:
  0.0 35.4 jit_solution(9146875017477104938)
XLA Ops:
  0.0 33.7 %shard_map.73 = bf16[192,512]{1,0:T(8,128)(2,1)} custom-call(bf16[192,512]{1,0:T(8,128)(2,1)} %tokens_hbm.1, s32[1,192]{1,0:T(1,128)} %bitcast.5, f32[1,512]{1,0:T(1,128)} %bitcast.3, bf16[512,2048]{1,0:T(8,128)(2,1)} %w_proj_hbm.1, f32[8,16]{1,0:T(8,128)} %bias_hbm.1, f32[1,512]{1,0:T(1,128)} %bitcast.4, bf16[512,512]{1,0:T(8,128)(2,1)} %w_out_hbm.1), custom_call_target="tpu_custom_call" | custom-call | tf_op jit(solution)/shard_map/pallas_call | solution.py:506
  33.8 1.6 %copy.9 = bf16[192,512]{1,0:T(8,128)(2,1)} copy(bf16[192,512]{1,0:T(8,128)(2,1)} %shard_map.73) | data formatting | bytes 393216
where the time goes:
time: 35.5 us; the launch traced here: 35.4 us
  Pallas kernels  33.7 us (95%)
  local copies, waits for them, and re-layouts  1.62 us (5%)
    pallas_call x1, Pallas kernels, body(): pl.pallas_call(functools.partial(kernel, parts, heads), out_shape=jax.Sha...  33.7 us
    unnamed x1, local copies, waits for them, and re-layouts  1.62 us

commit v1 on v0

--- a/solution.py
+++ b/solution.py
@@ -15,6 +15,32 @@
     centered = values - jnp.mean(values, axis=-1, keepdims=True)
     spread = jnp.mean(centered * centered, axis=-1, keepdims=True)
     return centered * lax.rsqrt(spread + EPSILON) * gain
+
+
+LANE_LOOKUP = lax.GatherDimensionNumbers(
+    offset_dims=(),
+    collapsed_slice_dims=(1,),
+    start_index_map=(1,),
+    operand_batching_dims=(0,),
+    start_indices_batching_dims=(0,),
+)
+ROW_LOOKUP = lax.GatherDimensionNumbers(
+    offset_dims=(),
+    collapsed_slice_dims=(1,),
+    start_index_map=(1,),
+    operand_batching_dims=(0, 2),
+    start_indices_batching_dims=(0, 2),
+)
+
+
+def look_up(table, index, dimensions):
+    return lax.gather(
+        table,
+        index[..., None],
+        dimensions,
+        (1,) * table.ndim,
+        mode=lax.GatherScatterMode.PROMISE_IN_BOUNDS,
+    )
 
 
 def kernel(
@@ -202,13 +228,30 @@
     gate_buf[...] = jax.nn.silu(gate_proj).astype(jnp.bfloat16)
     total_buf[...] = jnp.zeros_like(total_buf)
 
-    zeros_count = lax.broadcasted_iota(jnp.int32, (8, LANES), 1)
-    bucket = jnp.clip((33 - zeros_count) >> 1, 0, buckets - 1)
-    table = jnp.zeros((8, LANES), jnp.float32)
-    for bucket_id in range(buckets):
-        table = jnp.where(bucket == bucket_id, 0.5 * bias_ref[my_head, bucket_id], table)
-    table_two = jnp.broadcast_to(table[:1], (2 * rows, LANES))
-    table = table_two[:rows]
+    def half_bias(bucket):
+        table = jnp.zeros((8, LANES), jnp.float32)
+        for bucket_id in range(buckets):
+            table = jnp.where(bucket == bucket_id, 0.5 * bias_ref[my_head, bucket_id], table)
+        return table
+
+    lane_id = lax.broadcasted_iota(jnp.int32, (8, LANES), 1)
+    lane_table = half_bias(jnp.clip((33 - lane_id) >> 1, 0, buckets - 1))[:1]
+    place_id = lax.broadcasted_iota(jnp.int32, (8, LANES), 0)
+    far_table = half_bias(jnp.where(place_id == 0, 8, 16 - place_id))
+    close_table = half_bias(jnp.where(place_id == 0, 0, 8 - place_id))
+
+    def bias_of(elapsed, by_rows):
+        if not by_rows:
+            table = jnp.broadcast_to(lane_table, elapsed.shape)
+            return look_up(table, lax.clz(elapsed), LANE_LOOKUP)
+        tiles = (elapsed.shape[0] // 8, 8, LANES)
+        zeros_count = lax.clz(jnp.minimum(elapsed, 2**30 - 1))
+        index = ((zeros_count >> 1) & 7).reshape(tiles)
+        far_bias = look_up(jnp.broadcast_to(far_table[None], tiles), index, ROW_LOOKUP)
+        close_bias = look_up(jnp.broadcast_to(close_table[None], tiles), index, ROW_LOOKUP)
+        return jnp.where(
+            elapsed >= 4**7, far_bias.reshape(elapsed.shape), close_bias.reshape(elapsed.shape)
+        )
 
     def wait_stamps(step, carry):
         source = lax.rem(me + step, parts)
@@ -268,84 +311,57 @@
             [jnp.where(low, packed, 0.0), jnp.where(low, pltpu.roll(packed, head_size, 1), 0.0)], axis=0
         ).astype(jnp.bfloat16)
 
-    row_id = lax.broadcasted_iota(jnp.int32, (rows, LANES), 0)
-    col_id = lax.broadcasted_iota(jnp.int32, (rows, LANES), 1)
-
-    def visit_tile(slot, block, tile, masked):
+    chunk = 64
+    row_id = lax.broadcasted_iota(jnp.int32, (chunk, LANES), 0)
+    col_id = lax.broadcasted_iota(jnp.int32, (chunk, LANES), 1)
+    spread = col_id - row_id
+
+    def visit_tile(slot, count, tile, masked):
         key_value = kv_all[pl.ds(tile * blocks_per_tile, blocks_per_tile)]
         key_value = key_value.reshape(key_tile, LANES)
+        queries = query_buf[pl.ds(slot, count)].reshape(count * rows, LANES)
         scores = lax.dot_general(
-            query_buf[slot], key_value, (((1,), (1,)), ((), ())), preferred_element_type=jnp.float32
-        )
-        query_stamp = stamp_rows[slot]
+            queries, key_value, (((1,), (1,)), ((), ())), preferred_element_type=jnp.float32
+        )
         weights = []
         for first in range(0, key_tile, LANES):
-            elapsed = query_stamp - stamp_keys[tile, :, first : first + LANES]
-            bias = jnp.take_along_axis(table, lax.clz(elapsed), axis=1, mode="promise_in_bounds")
-            halved = scores[:, first : first + LANES] + bias
-            weight = halved + halved * jnp.tanh(halved)
-            if masked:
-                ahead = tile * key_tile + first - block * rows
-                weight = jnp.where(col_id + ahead <= row_id, weight, 0.0)
-            weights.append(weight.astype(jnp.bfloat16))
-        total_buf[slot] += jnp.dot(
+            column = []
+            for top in range(0, count * rows, chunk):
+                place, start = top // rows, top % rows
+                query_stamp = stamp_rows[slot + place, start : start + chunk]
+                elapsed = query_stamp - stamp_keys[tile, :, first : first + LANES]
+                bias = bias_of(elapsed, (top // chunk + first // LANES) % 3 != 0)
+                halved = scores[top : top + chunk, first : first + LANES] + bias
+                halved = halved.astype(jnp.bfloat16)
+                weight = halved + halved * jnp.tanh(halved)
+                if masked and place == 0:
+                    ahead = tile * key_tile + first - block_of(slot, my_split) * rows - start
+                    weight = jnp.where(spread <= -ahead, weight.astype(jnp.float32), 0.0)
+                    weight = weight.astype(jnp.bfloat16)
+                column.append(weight)
+            weights.append(jnp.concatenate(column, axis=0))
+        sums = jnp.dot(
             jnp.concatenate(weights, axis=1), key_value, preferred_element_type=jnp.float32
         )
-
-    def visit_two(slot, group):
+        total_buf[pl.ds(slot, count)] += sums.reshape(count, rows, LANES)
+
+    def visit(slot, count, group, masked):
+        if group_tiles == 1:
+            visit_tile(slot, count, group, masked)
+            return
+
         def one(tile, carry):
-            key_value = kv_all[pl.ds(tile * blocks_per_tile, blocks_per_tile)]
-            key_value = key_value.reshape(key_tile, LANES)
-            queries = query_buf[pl.ds(slot, 2)].reshape(2 * rows, LANES)
-            query_stamp = stamp_rows[pl.ds(slot, 2)].reshape(2 * rows, LANES)
-            scores = lax.dot_general(
-                queries, key_value, (((1,), (1,)), ((), ())), preferred_element_type=jnp.float32
-            )
-            weights = []
-            for first in range(0, key_tile, LANES):
-                elapsed = query_stamp - stamp_keys[tile, :, first : first + LANES]
-                bias = jnp.take_along_axis(table_two, lax.clz(elapsed), axis=1, mode="promise_in_bounds")
-                halved = scores[:, first : first + LANES] + bias
-                weights.append((halved + halved * jnp.tanh(halved)).astype(jnp.bfloat16))
-            sums = jnp.dot(
-                jnp.concatenate(weights, axis=1), key_value, preferred_element_type=jnp.float32
-            )
-            total_buf[pl.ds(slot, 2)] += sums.reshape(2, rows, LANES)
+            visit_tile(slot, count, tile, masked)
             return carry
 
         lax.fori_loop(group * group_tiles, (group + 1) * group_tiles, one, 0)
 
-    def visit_later(first, end, group):
-        count = end - first
-
-        def two(step, carry):
-            visit_two(first + 2 * step, group)
-            return carry
-
-        lax.fori_loop(0, count // 2, two, 0)
-
-        @pl.when(count % 2 == 1)
-        def _():
-            visit_before(end - 1, group)
-
-    def visit_before(slot, group):
-        def one(tile, carry):
-            visit_tile(slot, 0, tile, False)
-            return carry
-
-        lax.fori_loop(group * group_tiles, (group + 1) * group_tiles, one, 0)
-
-    def visit_own(slot):
-        block = block_of(slot, my_split)
-        last = block // blocks_per_tile
-
-        def one(tile, carry):
-            visit_tile(slot, block, tile, False)
-            return carry
-
-        if group_tiles > 1:
-            lax.fori_loop(slot * group_tiles, last, one, 0)
-        visit_tile(slot, block, last, True)
+    def visit_wedge(group, first):
+        for offset in range(near):
+
+            @pl.when(group - first == offset)
+            def _():
+                visit(group, near - offset, group, True)
 
     def send_back(slot, target):
         return remote(
@@ -375,60 +391,54 @@
 
     lax.fori_loop(near_first, near_first + near, take_near, 0)
 
-    def near_group(group, carry):
-        take_forwarded(group)
-        visit_own(group)
-
-        visit_later(group + 1, near_first + near, group)
-        return carry
-
-    lax.fori_loop(near_first, near_first + near, near_group, 0)
-
     lower_end = near * (1 - upper)
-    lax.fori_loop(0, lower_end, finish, 0)
+
+    def far_at(step):
+        return far_first + lax.rem(my_place - step + near, near)
+
+    def stage(step, carry):
+        turn, place = step // near, step % near
+
+        @pl.when(step == near)
+        def _():
+            lax.fori_loop(0, lower_end, finish, 0)
+            lax.fori_loop(far_first, far_first + near, far_query, 0)
+
+        far = turn == 2
+        group = jnp.where(far, far_at(place), place + jnp.where(turn == 0, near_first, 0))
+
+        @pl.when(step == 2 * near)
+        def _():
+            take_direct(far_at(0))
+
+        @pl.when(step == 3 * near - 1)
+        def _():
+            lax.fori_loop(lower_end, group, finish, 0)
+
+        @pl.when(turn != 1)
+        def _():
+            take_forwarded(group)
+
+        @pl.when(far & (place + 1 < near))
+        def _():
+            take_direct(far_at(place + 1))
+
+        @pl.when(turn != 1)
+        def _():
+            visit_wedge(group, jnp.where(far, far_first, near_first))
+
+        @pl.when(turn == 2 - (1 - upper))
+        def _():
+            visit(near, near, group, False)
+
+        return carry
 
     def far_query(slot, carry):
         take_query(slot)
         return carry
 
-    lax.fori_loop(far_first, far_first + near, far_query, 0)
-
-    def later_queries(group, carry):
-        visit_later(near, slots, group)
-        return carry
-
-    lax.fori_loop(0, lower_end, later_queries, 0)
-
-    def far_at(step):
-        return far_first + lax.rem(my_place - step + near, near)
-
-    take_direct(far_at(0))
-
-    def far_group(step, carry):
-        group = far_at(step)
-        take_forwarded(group)
-
-        @pl.when(step + 1 < near)
-        def _():
-            take_direct(far_at(step + 1))
-
-        visit_own(group)
-        visit_later(group + 1, slots, group)
-        return carry
-
-    lax.fori_loop(0, near - 1, far_group, 0)
-
-    last_group = far_at(near - 1)
-    lax.fori_loop(lower_end, last_group, finish, 0)
-    take_forwarded(last_group)
-    visit_own(last_group)
-    finish(last_group, 0)
-
-    def last_one(slot, carry):
-        visit_before(slot, last_group)
-        return finish(slot, carry)
-
-    lax.fori_loop(last_group + 1, slots, last_one, 0)
+    lax.fori_loop(0, 3 * near, stage, 0)
+    lax.fori_loop(far_at(near - 1), slots, finish, 0)
 
     def drain_both(head, target):
         q_copy(head, target).wait_send()

time: 35.5 us -> 33.4 us (0.941)
  Pallas kernels: 33.7 us -> 31.6 us
    pallas_call x1, Pallas kernels: 33.7 us -> 31.6 us  [body(): pl.pallas_call(functools.partial(kernel, parts, heads), out_shape=jax.Sha...]
where the time goes in v1:
time: 33.4 us; the launch traced here: 33.2 us
  Pallas kernels  31.6 us (95%)
  local copies, waits for them, and re-layouts  1.62 us (5%)
    pallas_call x1, Pallas kernels, body(): pl.pallas_call(functools.partial(kernel, parts, heads), out_shape=jax.Sha...  31.6 us
    unnamed x1, local copies, waits for them, and re-layouts  1.62 us

profile of v1, /device:TPU:0, one launch (start us, length us, event | category | flops | bytes accessed | tf_op | source)
XLA Modules:
  0.0 33.2 jit_solution(9666975358228365473)
XLA Ops:
  0.0 31.6 %shard_map.73 = bf16[192,512]{1,0:T(8,128)(2,1)} custom-call(bf16[192,512]{1,0:T(8,128)(2,1)} %tokens_hbm.1, s32[1,192]{1,0:T(1,128)} %bitcast.5, f32[1,512]{1,0:T(1,128)} %bitcast.3, bf16[512,2048]{1,0:T(8,128)(2,1)} %w_proj_hbm.1, f32[8,16]{1,0:T(8,128)} %bias_hbm.1, f32[1,512]{1,0:T(1,128)} %bitcast.4, bf16[512,512]{1,0:T(8,128)(2,1)} %w_out_hbm.1), custom_call_target="tpu_custom_call" | custom-call | tf_op jit(solution)/shard_map/pallas_call | solution.py:516
  31.6 1.6 %copy.9 = bf16[192,512]{1,0:T(8,128)(2,1)} copy(bf16[192,512]{1,0:T(8,128)(2,1)} %shard_map.73) | data formatting | bytes 393216

commit v2 on v1

v2 whole, which is shorter than its diff:
```python
import functools

import jax
import jax.numpy as jnp
from jax import lax
from jax.experimental import pallas as pl
from jax.experimental.pallas import tpu as pltpu
from jax.sharding import PartitionSpec as P

EPSILON = 1e-05
LANES = 128


def layer_norm(values, gain):
    centered = values - jnp.mean(values, axis=-1, keepdims=True)
    spread = jnp.mean(centered * centered, axis=-1, keepdims=True)
    return centered * lax.rsqrt(spread + EPSILON) * gain


LANE_LOOKUP = lax.GatherDimensionNumbers(
    offset_dims=(),
    collapsed_slice_dims=(1,),
    start_index_map=(1,),
    operand_batching_dims=(0,),
    start_indices_batching_dims=(0,),
)
ROW_LOOKUP = lax.GatherDimensionNumbers(
    offset_dims=(),
    collapsed_slice_dims=(1,),
    start_index_map=(1,),
    operand_batching_dims=(0, 2),
    start_indices_batching_dims=(0, 2),
)


def look_up(table, index, dimensions):
    return lax.gather(
        table,
        index[..., None],
        dimensions,
        (1,) * table.ndim,
        mode=lax.GatherScatterMode.PROMISE_IN_BOUNDS,
    )


def kernel(
    parts,
    heads,
    tokens_hbm,
    stamps_hbm,
    norm_gain_hbm,
    w_proj_hbm,
    bias_hbm,
    attn_gain_hbm,
    w_out_hbm,
    out_ref,
    tokens_ref,
    stamps_ref,
    norm_gain_ref,
    w_proj_ref,
    bias_ref,
    attn_gain_ref,
    w_out_ref,
    kv_send,
    q_send,
    kv_all,
    q_all,
    query_buf,
    stamp_all,
    stamp_keys,
    stamp_rows,
    total_buf,
    gate_buf,
    back_buf,
    att_buf,
    part_buf,
    load_sem,
    kv_send_sem,
    q_send_sem,
    far_send_sem,
    fwd_sem,
    kv_sem,
    q_sem,
    stamp_send_sem,
    stamp_sem,
    back_sem,
    att_sem,
    part_sem,
):
    rows, width = tokens_ref.shape
    half = rows // 2
    head_size = width // heads
    splits = parts // heads
    near = heads // 2
    side = parts // 2
    blocks_per_tile = max(1, 384 // rows)
    key_tile = blocks_per_tile * rows
    group_tiles = splits // blocks_per_tile
    buckets = bias_ref.shape[1]

    loads = [
        pltpu.make_async_copy(source, target, load_sem.at[index])
        for index, (source, target) in enumerate(
            [
                (tokens_hbm, tokens_ref),
                (norm_gain_hbm, norm_gain_ref),
                (w_proj_hbm.at[:, width:], w_proj_ref.at[:, width:]),
                (stamps_hbm, stamps_ref),
                (bias_hbm, bias_ref),
                (w_proj_hbm.at[:, :width], w_proj_ref.at[:, :width]),
                (attn_gain_hbm, attn_gain_ref),
                (w_out_hbm, w_out_ref),
            ]
        )
    ]
    for load in loads:
        load.start()

    me = lax.axis_index("pb")
    my_group = me // splits
    my_split = me % splits
    upper = my_group // near
    my_place = my_group % near
    near_first = upper * near
    far_first = near - near_first
    side_first = upper * side

    def split_of(block):
        place = block % splits
        odd = (block // splits) % 2
        return place + odd * (splits - 1 - 2 * place)

    def block_of(slot, split):
        odd = slot % 2
        return slot * splits + split + odd * (splits - 1 - 2 * split)

    def remote(source, target, send, receive, device):
        return pltpu.make_async_remote_copy(
            src_ref=source,
            dst_ref=target,
            send_sem=send,
            recv_sem=receive,
            device_id={"pb": device},
            device_id_type=pl.DeviceIdType.MESH,
        )

    barrier = pltpu.get_barrier_semaphore()

    def greet(step, carry):
        other = lax.rem(me + step, parts)
        pl.semaphore_signal(
            barrier, inc=1, device_id={"pb": other}, device_id_type=pl.DeviceIdType.MESH
        )
        return carry

    lax.fori_loop(1, parts, greet, 0)

    low = lax.broadcasted_iota(jnp.int32, (1, LANES), 1) < head_size

    for load in loads[:3]:
        load.wait()
    normed = layer_norm(tokens_ref[...].astype(jnp.float32), norm_gain_ref[...]).astype(jnp.bfloat16)
    front = jnp.dot(normed, w_proj_ref[:, width : 2 * width], preferred_element_type=jnp.float32)
    scaled = front.astype(jnp.bfloat16).astype(jnp.float32) * (0.5 * head_size ** (-0.5))
    back = jnp.dot(normed, w_proj_ref[:, 2 * width :], preferred_element_type=jnp.float32)
    for pair in range(near):
        cols = slice(pair * LANES, (pair + 1) * LANES)
        key_cols = back[:, :width][:, cols]
        value_cols = back[:, width:][:, cols]
        query_cols = scaled[:, cols]
        kv_send[pair, 0] = jnp.where(
            low, key_cols, pltpu.roll(value_cols, head_size, 1)
        ).astype(jnp.bfloat16)
        kv_send[pair, 1] = jnp.where(
            low, pltpu.roll(key_cols, head_size, 1), value_cols
        ).astype(jnp.bfloat16)
        top, bottom = query_cols[:half], query_cols[half:]
        q_send[pair, 0] = jnp.where(low, top, pltpu.roll(bottom, head_size, 1)).astype(jnp.bfloat16)
        q_send[pair, 1] = jnp.where(low, pltpu.roll(top, head_size, 1), bottom).astype(jnp.bfloat16)
    loads[3].wait()
    loads[4].wait()

    my_home = split_of(me)

    def stamp_copy(target):
        return remote(
            stamps_ref, stamp_all.at[me], stamp_send_sem.at[target], stamp_sem.at[me], target
        )

    def kv_copy(place, target):
        return remote(kv_send.at[place], kv_all.at[me], kv_send_sem.at[place], kv_sem.at[me], target)

    def q_copy(place, target):
        return remote(
            q_send.at[place], q_all.at[my_group], q_send_sem.at[place], q_sem.at[my_group], target
        )

    def late_kv_copy(place, target):
        return remote(
            kv_send.at[place, 1], kv_all.at[me, 1], far_send_sem.at[place], kv_sem.at[me], target
        )

    def early_q_copy(place, target):
        return remote(
            q_send.at[place, 0], q_all.at[my_group, 0], far_send_sem.at[place], q_sem.at[my_group], target
        )

    def each_near(act):
        def one(step, carry):
            place = lax.rem(my_place + step, near)
            target = (near_first + place) * splits + my_home

            @pl.when(target != me)
            def _():
                act(place, target)

            return carry

        lax.fori_loop(0, near, one, 0)

    def each_far(act):
        def one(step, carry):
            place = lax.rem(my_place + step, near)
            target = (far_first + place) * splits + my_home

            @pl.when(upper == 0)
            def _():
                act(late_kv_copy(place, target))

            @pl.when(upper == 1)
            def _():
                act(early_q_copy(place, target))

            return carry

        lax.fori_loop(0, near, one, 0)

    def near_peer(step):
        return side_first + lax.rem(me - side_first + step, side)

    def far_peer(step):
        return side - side_first + lax.rem(me - side_first + step, side)

    def send_near_stamps(step, carry):
        stamp_copy(near_peer(step)).start()
        return carry

    def send_far_stamps(step, carry):
        stamp_copy(far_peer(step)).start()
        return carry

    def start_both(place, target):
        q_copy(place, target).start()
        kv_copy(place, target).start()

    pl.semaphore_wait(barrier, parts - 1)
    lax.fori_loop(1, side, send_near_stamps, 0)
    each_near(start_both)
    lax.fori_loop(0, side, send_far_stamps, 0)
    each_far(lambda copy: copy.start())

    stamp_all[me] = stamps_ref[...]

    @pl.when(my_home == my_split)
    def _():
        kv_all[me] = kv_send[my_place]
        q_all[my_group] = q_send[my_place]

    @pl.when(upper == 0)
    def _():
        part_buf[...] = jnp.zeros_like(part_buf)

    loads[5].wait()
    gate_proj = jnp.dot(normed, w_proj_ref[:, :width], preferred_element_type=jnp.float32)
    gate_buf[...] = jax.nn.silu(gate_proj).astype(jnp.bfloat16)
    total_buf[...] = jnp.zeros_like(total_buf)

    lane_id = lax.broadcasted_iota(jnp.int32, (8, LANES), 1)
    place_id = lax.broadcasted_iota(jnp.int32, (8, LANES), 0)

    def tables_of(head):
        def half_bias(bucket):
            table = jnp.zeros((8, LANES), jnp.float32)
            for bucket_id in range(buckets):
                table = jnp.where(bucket == bucket_id, 0.5 * bias_ref[head, bucket_id], table)
            return table

        return (
            half_bias(jnp.clip((33 - lane_id) >> 1, 0, buckets - 1))[:1],
            half_bias(jnp.where(place_id == 0, 8, 16 - place_id)),
            half_bias(jnp.where(place_id == 0, 0, 8 - place_id)),
        )

    near_tables = [tables_of(2 * my_place), tables_of(2 * my_place + 1)]
    square_tables = [tables_of(2 * my_place + upper)]

    def biases_of(elapsed, tables, by_rows):
        if not by_rows:
            index = lax.clz(elapsed)
            return [look_up(jnp.broadcast_to(lane, elapsed.shape), index, LANE_LOOKUP) for lane, _, _ in tables]
        tiles = (elapsed.shape[0] // 8, 8, LANES)
        zeros_count = lax.clz(jnp.minimum(elapsed, 2**30 - 1))
        index = ((zeros_count >> 1) & 7).reshape(tiles)
        old = elapsed >= 4**7
        biases = []
        for _, far_table, close_table in tables:
            far_bias = look_up(jnp.broadcast_to(far_table[None], tiles), index, ROW_LOOKUP)
            close_bias = look_up(jnp.broadcast_to(close_table[None], tiles), index, ROW_LOOKUP)
            biases.append(
                jnp.where(old, far_bias.reshape(elapsed.shape), close_bias.reshape(elapsed.shape))
            )
        return biases

    def wait_stamps(source):
        remote(
            stamps_ref, stamp_all.at[source], stamp_send_sem.at[source], stamp_sem.at[source], source
        ).wait_recv()

    def wait_near_stamps(step, carry):
        wait_stamps(near_peer(step))
        return carry

    def wait_far_stamps(step, carry):
        wait_stamps(far_peer(step))
        return carry

    def join_stamps(tile, carry):
        stamp_keys[tile] = jnp.concatenate(
            [stamp_all[tile * blocks_per_tile + place] for place in range(blocks_per_tile)], axis=1
        )
        return carry

    def turn_stamps(slot, carry):
        block = block_of(slot, my_split)
        stamp_rows[slot] = jnp.transpose(jnp.broadcast_to(stamp_all[block], (LANES, rows)))
        return carry

    lax.fori_loop(1, side, wait_near_stamps, 0)
    lax.fori_loop(near_first * group_tiles, (near_first + near) * group_tiles, join_stamps, 0)
    lax.fori_loop(near_first, near_first + near, turn_stamps, 0)

    def forward(slot, source, step):
        peer = my_group * splits + lax.rem(my_split + step, splits)
        return remote(
            kv_all.at[source], kv_all.at[source], fwd_sem.at[slot, step], kv_sem.at[source], peer
        )

    def late_forward(slot, source, step):
        peer = my_group * splits + lax.rem(my_split + step, splits)
        return remote(
            kv_all.at[source, 1], kv_all.at[source, 1], fwd_sem.at[slot, step], kv_sem.at[source], peer
        )

    def take_direct(slot):
        source = block_of(slot, my_split)

        @pl.when(source != me)
        def _():
            remote(
                kv_send.at[0], kv_all.at[source], kv_send_sem.at[0], kv_sem.at[source], source
            ).wait_recv()

        for step in range(1, splits):
            forward(slot, source, step).start()

    def take_forwarded(slot):
        for step in range(1, splits):
            source = block_of(slot, lax.rem(my_split + step, splits))
            forward(slot, source, step).wait_recv()

    def take_late_direct(slot):
        source = block_of(slot, my_split)
        remote(
            kv_send.at[0, 1], kv_all.at[source, 1], far_send_sem.at[0], kv_sem.at[source], source
        ).wait_recv()
        for step in range(1, splits):
            late_forward(slot, source, step).start()

    def take_late_forwarded(slot):
        for step in range(1, splits):
            source = block_of(slot, lax.rem(my_split + step, splits))
            late_forward(slot, source, step).wait_recv()

    def unpack(packed):
        packed = packed.astype(jnp.float32)
        return jnp.concatenate(
            [jnp.where(low, packed, 0.0), jnp.where(low, pltpu.roll(packed, head_size, 1), 0.0)], axis=0
        ).astype(jnp.bfloat16)

    def take_query(slot):
        source = block_of(slot, my_split)

        @pl.when(source != me)
        def _():
            remote(
                q_send.at[0], q_all.at[slot], q_send_sem.at[0], q_sem.at[slot], source
            ).wait_recv()

        for head in range(2):
            query_buf[head, slot - near_first] = unpack(q_all[slot, head])

    def take_far_query(slot, carry):
        source = block_of(slot, my_split)
        remote(
            q_send.at[0, 0], q_all.at[slot, 0], far_send_sem.at[0], q_sem.at[slot], source
        ).wait_recv()
        query_buf[2, slot - near] = unpack(q_all[slot, 0])
        return carry

    chunk = 64
    row_id = lax.broadcasted_iota(jnp.int32, (chunk, LANES), 0)
    col_id = lax.broadcasted_iota(jnp.int32, (chunk, LANES), 1)
    spread = col_id - row_id

    def visit_tile(slot, count, tile, jobs, tables, masked):
        unit = slot - jnp.where(slot >= near, near, 0)
        key_values, scores = [], []
        for query_head, key_head in jobs:
            key_value = kv_all[pl.ds(tile * blocks_per_tile, blocks_per_tile), key_head]
            key_values.append(key_value.reshape(key_tile, LANES))
            queries = query_buf[query_head, pl.ds(unit, count)].reshape(count * rows, LANES)
            scores.append(
                lax.dot_general(
                    queries,
                    key_values[-1],
                    (((1,), (1,)), ((), ())),
                    preferred_element_type=jnp.float32,
                )
            )
        weights = [[] for _ in jobs]
        for first in range(0, key_tile, LANES):
            columns = [[] for _ in jobs]
            for top in range(0, count * rows, chunk):
                place, start = top // rows, top % rows
                query_stamp = stamp_rows[slot + place, start : start + chunk]
                elapsed = query_stamp - stamp_keys[tile, :, first : first + LANES]
                biases = biases_of(elapsed, tables, (top // chunk + first // LANES) % 3 != 0)
                for score, bias, column in zip(scores, biases, columns):
                    halved = score[top : top + chunk, first : first + LANES] + bias
                    halved = halved.astype(jnp.bfloat16)
                    weight = halved + halved * jnp.tanh(halved)
                    if masked and place == 0:
                        ahead = tile * key_tile + first - block_of(slot, my_split) * rows - start
                        weight = jnp.where(spread <= -ahead, weight.astype(jnp.float32), 0.0)
                        weight = weight.astype(jnp.bfloat16)
                    column.append(weight)
            for weight, column in zip(weights, columns):
                weight.append(jnp.concatenate(column, axis=0))
        for (query_head, _), weight, key_value in zip(jobs, weights, key_values):
            sums = jnp.dot(
                jnp.concatenate(weight, axis=1), key_value, preferred_element_type=jnp.float32
            )
            total_buf[query_head, pl.ds(unit, count)] += sums.reshape(count, rows, LANES)

    def visit(slot, count, group, jobs, tables, masked):
        if group_tiles == 1:
            visit_tile(slot, count, group, jobs, tables, masked)
            return

        def one(tile, carry):
            visit_tile(slot, count, tile, jobs, tables, masked)
            return carry

        lax.fori_loop(group * group_tiles, (group + 1) * group_tiles, one, 0)

    def visit_near(slot, count, group, masked):
        visit(slot, count, group, [(0, 0), (1, 1)], near_tables, masked)

    def back_copy(kind, unit):
        slot = unit + (near if kind == 2 else near_first)
        target, semaphore = (
            (part_buf.at[my_place], part_sem.at[my_place])
            if kind == 2
            else (att_buf.at[2 * my_place + kind], att_sem.at[2 * my_place + kind])
        )
        block = block_of(slot, my_split)
        return block, remote(
            back_buf.at[kind, unit], target, back_sem.at[kind, unit], semaphore, block
        )

    def finish(kind):
        def one(unit, carry):
            block, copy = back_copy(kind, unit)
            total = total_buf[kind, unit]
            result = jnp.where(low, pltpu.roll(total[:half], head_size, 1), total[half:])
            result = result.astype(jnp.bfloat16)
            back_buf[kind, unit] = result
            if kind == 2:
                copy.start()
                return carry

            @pl.when(block == me)
            def _():
                att_buf[2 * my_place + kind] = result

            @pl.when(block != me)
            def _():
                copy.start()

            return carry

        lax.fori_loop(0, near, one, 0)

    def take_near(slot, carry):
        take_direct(slot)
        take_query(slot)
        return carry

    lax.fori_loop(near_first, near_first + near, take_near, 0)

    def near_group(group, carry):
        take_forwarded(group)
        rest = near_first + near - group

        @pl.when(rest == 1)
        def _():
            visit_near(group, 1, group, True)

        @pl.when(rest > 1)
        def _():
            visit_near(group, 2, group, True)

        def two(step, inner):
            visit_near(group + 2 + 2 * step, 2, group, False)
            return inner

        lax.fori_loop(0, (rest - 2) // 2, two, 0)

        @pl.when((rest > 2) & (rest % 2 == 1))
        def _():
            visit_near(group + rest - 1, 1, group, False)

        return carry

    lax.fori_loop(near_first, near_first + near, near_group, 0)
    finish(0)

    @pl.when(upper == 0)
    def _():
        finish(1)

    lax.fori_loop(0, side, wait_far_stamps, 0)

    @pl.when(upper == 0)
    def _():
        lax.fori_loop(near, 2 * near, turn_stamps, 0)
        lax.fori_loop(near, 2 * near, take_far_query, 0)

    def late_at(step):
        return lax.rem(my_place - step + near, near)

    @pl.when(upper == 1)
    def _():
        lax.fori_loop(0, near * group_tiles, join_stamps, 0)
        take_late_direct(late_at(0))

    def square(step, carry):
        group = late_at(step)

        @pl.when(upper == 1)
        def _():
            take_late_forwarded(group)

            @pl.when(step + 1 < near)
            def _():
                take_late_direct(late_at(step + 1))

        visit(near, near, group, [(2 - upper, upper)], square_tables, False)
        return carry

    lax.fori_loop(0, near, square, 0)

    @pl.when(upper == 0)
    def _():
        finish(2)

    @pl.when(upper == 1)
    def _():
        finish(1)

    def drain_both(place, target):
        q_copy(place, target).wait_send()
        kv_copy(place, target).wait_send()

    each_near(drain_both)
    each_far(lambda copy: copy.wait_send())

    def drain(step, carry):
        stamp_copy(lax.rem(me + step, parts)).wait_send()
        return carry

    lax.fori_loop(1, parts, drain, 0)

    def drain_near(slot, carry):
        for step in range(1, splits):
            forward(slot, block_of(slot, my_split), step).wait_send()
        return carry

    def drain_late(slot, carry):
        for step in range(1, splits):
            late_forward(slot, block_of(slot, my_split), step).wait_send()
        return carry

    def drain_back(kind):
        def one(unit, carry):
            block, copy = back_copy(kind, unit)

            @pl.when(block != me)
            def _():
                copy.wait_send()

            return carry

        lax.fori_loop(0, near, one, 0)

    lax.fori_loop(near_first, near_first + near, drain_near, 0)
    drain_back(0)
    drain_back(1)

    @pl.when(upper == 0)
    def _():
        drain_back(2)

    @pl.when(upper == 1)
    def _():
        lax.fori_loop(0, near, drain_late, 0)

    loads[6].wait()
    loads[7].wait()

    def take_back(step, carry):
        place = lax.rem(my_place + step, near)
        source = (near_first + place) * splits + my_home

        @pl.when(source != me)
        def _():
            for head in range(2):
                remote(
                    back_buf.at[0, 0],
                    att_buf.at[2 * place + head],
                    back_sem.at[0, 0],
                    att_sem.at[2 * place + head],
                    source,
                ).wait_recv()

        @pl.when(upper == 1)
        def _():
            remote(
                back_buf.at[0, 0],
                part_buf.at[place],
                back_sem.at[0, 0],
                part_sem.at[place],
                place * splits + my_home,
            ).wait_recv()

        return carry

    lax.fori_loop(0, near, take_back, 0)

    pieces = []
    for pair in range(near):
        even = att_buf[2 * pair].astype(jnp.float32) + part_buf[pair].astype(jnp.float32)
        odd = att_buf[2 * pair + 1].astype(jnp.float32)
        pieces.append(
            jnp.concatenate(
                [
                    jnp.where(low, even, pltpu.roll(odd, head_size, 1)),
                    jnp.where(low, pltpu.roll(even, head_size, 1), odd),
                ],
                axis=0,
            )
        )
    attended = jnp.concatenate(pieces, axis=1)
    gated = layer_norm(attended, attn_gain_ref[...]) * gate_buf[...].astype(jnp.float32)
    mixed = tokens_ref[...].astype(jnp.float32) + jnp.dot(
        gated.astype(jnp.bfloat16), w_out_ref[...], preferred_element_type=jnp.float32
    )
    out_ref[...] = mixed.astype(jnp.bfloat16)


def solution(mesh):
    parts = mesh.shape["pb"]

    def body(tokens, stamps, norm_gain, w_proj, rel_bias, attn_gain, w_out):
        rows, width = tokens.shape
        heads = rel_bias.shape[0]
        splits = parts // heads
        near = heads // 2
        blocks_per_tile = max(1, 384 // rows)
        vmem = pl.BlockSpec(memory_space=pltpu.VMEM)
        return pl.pallas_call(
            functools.partial(kernel, parts, heads),
            out_shape=jax.ShapeDtypeStruct((rows, width), jnp.bfloat16),
            in_specs=[pl.BlockSpec(memory_space=pltpu.HBM)] * 7,
            out_specs=vmem,
            scratch_shapes=[
                pltpu.VMEM((rows, width), jnp.bfloat16),
                pltpu.VMEM((1, rows), jnp.int32),
                pltpu.VMEM((1, width), jnp.float32),
                pltpu.VMEM(w_proj.shape, jnp.bfloat16),
                pltpu.SMEM(rel_bias.shape, jnp.float32),
                pltpu.VMEM((1, width), jnp.float32),
                pltpu.VMEM(w_out.shape, jnp.bfloat16),
                pltpu.VMEM((near, 2, rows, LANES), jnp.bfloat16),
                pltpu.VMEM((near, 2, rows // 2, LANES), jnp.bfloat16),
                pltpu.VMEM((parts, 2, rows, LANES), jnp.bfloat16),
                pltpu.VMEM((heads, 2, rows // 2, LANES), jnp.bfloat16),
                pltpu.VMEM((3, near, rows, LANES), jnp.bfloat16),
                pltpu.VMEM((parts, 1, rows), jnp.int32),
                pltpu.VMEM((parts // blocks_per_tile, 1, blocks_per_tile * rows), jnp.int32),
                pltpu.VMEM((heads, rows, LANES), jnp.int32),
                pltpu.VMEM((3, near, rows, LANES), jnp.float32),
                pltpu.VMEM((rows, width), jnp.bfloat16),
                pltpu.VMEM((3, near, rows // 2, LANES), jnp.bfloat16),
                pltpu.VMEM((heads, rows // 2, LANES), jnp.bfloat16),
                pltpu.VMEM((near, rows // 2, LANES), jnp.bfloat16),
                pltpu.SemaphoreType.DMA((8,)),
                pltpu.SemaphoreType.DMA((near,)),
                pltpu.SemaphoreType.DMA((near,)),
                pltpu.SemaphoreType.DMA((near,)),
                pltpu.SemaphoreType.DMA((heads, splits)),
                pltpu.SemaphoreType.DMA((parts,)),
                pltpu.SemaphoreType.DMA((heads,)),
                pltpu.SemaphoreType.DMA((parts,)),
                pltpu.SemaphoreType.DMA((parts,)),
                pltpu.SemaphoreType.DMA((3, near)),
                pltpu.SemaphoreType.DMA((heads,)),
                pltpu.SemaphoreType.DMA((near,)),
            ],
            compiler_params=pltpu.CompilerParams(
                collective_id=0, has_side_effects=True
            ),
        )(
            tokens,
            stamps.reshape(1, rows),
            norm_gain.reshape(1, width),
            w_proj,
            rel_bias,
            attn_gain.reshape(1, width),
            w_out,
        )

    return jax.shard_map(
        body,
        mesh=mesh,
        in_specs=(P(("groups", "pb"), None), P(("groups", "pb")), P(), P(), P(), P(), P()),
        out_specs=P(("groups", "pb"), None),
        check_vma=False,
    )
```

time: 33.4 us -> 31.4 us (0.940)
  the two profiles are of different devices: /device:TPU:0 before, /device:TPU:25 now
where the time goes in v2:
time: 31.4 us; the launch traced here: 31.2 us
  Pallas kernels  29.6 us (94%)
  local copies, waits for them, and re-layouts  1.62 us (5%)
    pallas_call x1, Pallas kernels, body(): pl.pallas_call(functools.partial(kernel, parts, heads), out_shape=jax.Sha...  29.6 us
    unnamed x1, local copies, waits for them, and re-layouts  1.62 us

profile of v2, /device:TPU:25, one launch (start us, length us, event | category | flops | bytes accessed | tf_op | source)
XLA Modules:
  0.0 31.2 jit_solution(7266645675029723220)
XLA Ops:
  0.0 29.6 %shard_map.73 = bf16[192,512]{1,0:T(8,128)(2,1)} custom-call(bf16[192,512]{1,0:T(8,128)(2,1)} %tokens_hbm.1, s32[1,192]{1,0:T(1,128)} %bitcast.5, f32[1,512]{1,0:T(1,128)} %bitcast.3, bf16[512,2048]{1,0:T(8,128)(2,1)} %w_proj_hbm.1, f32[8,16]{1,0:T(8,128)} %bias_hbm.1, f32[1,512]{1,0:T(1,128)} %bitcast.4, bf16[512,512]{1,0:T(8,128)(2,1)} %w_out_hbm.1), custom_call_target="tpu_custom_call" | custom-call | tf_op jit(solution)/shard_map/pallas_call | solution.py:691
  29.6 1.6 %copy.9 = bf16[192,512]{1,0:T(8,128)(2,1)} copy(bf16[192,512]{1,0:T(8,128)(2,1)} %shard_map.73) | data formatting | bytes 393216

commit v3 on v2

--- a/solution.py
+++ b/solution.py
@@ -86,6 +86,7 @@
     back_sem,
     att_sem,
     part_sem,
+    far_ready,
 ):
     rows, width = tokens_ref.shape
     half = rows // 2
@@ -146,14 +147,23 @@
 
     barrier = pltpu.get_barrier_semaphore()
 
+    def signal(semaphore, other):
+        pl.semaphore_signal(
+            semaphore, inc=1, device_id={"pb": other}, device_id_type=pl.DeviceIdType.MESH
+        )
+
+    def near_peer(step):
+        return side_first + lax.rem(me - side_first + step, side)
+
+    def far_peer(step):
+        return side - side_first + lax.rem(me - side_first + step, side)
+
     def greet(step, carry):
-        other = lax.rem(me + step, parts)
-        pl.semaphore_signal(
-            barrier, inc=1, device_id={"pb": other}, device_id_type=pl.DeviceIdType.MESH
-        )
-        return carry
-
-    lax.fori_loop(1, parts, greet, 0)
+        signal(barrier, near_peer(step))
+        return carry
+
+    lax.fori_loop(1, side, greet, 0)
+    signal(barrier, far_peer(0))
 
     low = lax.broadcasted_iota(jnp.int32, (1, LANES), 1) < head_size
 
@@ -218,9 +228,13 @@
 
         lax.fori_loop(0, near, one, 0)
 
+    def far_place(step):
+        place = step + (my_place % 2) * (1 - 2 * (step % 2))
+        return place + upper * (near - 1 - 2 * place)
+
     def each_far(act):
         def one(step, carry):
-            place = lax.rem(my_place + step, near)
+            place = far_place(step)
             target = (far_first + place) * splits + my_home
 
             @pl.when(upper == 0)
@@ -235,12 +249,6 @@
 
         lax.fori_loop(0, near, one, 0)
 
-    def near_peer(step):
-        return side_first + lax.rem(me - side_first + step, side)
-
-    def far_peer(step):
-        return side - side_first + lax.rem(me - side_first + step, side)
-
     def send_near_stamps(step, carry):
         stamp_copy(near_peer(step)).start()
         return carry
@@ -253,11 +261,15 @@
         q_copy(place, target).start()
         kv_copy(place, target).start()
 
-    pl.semaphore_wait(barrier, parts - 1)
+    pl.semaphore_wait(barrier, side)
+
+    def pass_on(step, carry):
+        signal(far_ready, near_peer(step))
+        return carry
+
+    lax.fori_loop(1, side, pass_on, 0)
     lax.fori_loop(1, side, send_near_stamps, 0)
     each_near(start_both)
-    lax.fori_loop(0, side, send_far_stamps, 0)
-    each_far(lambda copy: copy.start())
 
     stamp_all[me] = stamps_ref[...]
 
@@ -274,6 +286,10 @@
     gate_proj = jnp.dot(normed, w_proj_ref[:, :width], preferred_element_type=jnp.float32)
     gate_buf[...] = jax.nn.silu(gate_proj).astype(jnp.bfloat16)
     total_buf[...] = jnp.zeros_like(total_buf)
+
+    pl.semaphore_wait(far_ready, side - 1)
+    lax.fori_loop(0, side, send_far_stamps, 0)
+    each_far(lambda copy: copy.start())
 
     lane_id = lax.broadcasted_iota(jnp.int32, (8, LANES), 1)
     place_id = lax.broadcasted_iota(jnp.int32, (8, LANES), 0)
@@ -412,59 +428,77 @@
     col_id = lax.broadcasted_iota(jnp.int32, (chunk, LANES), 1)
     spread = col_id - row_id
 
-    def visit_tile(slot, count, tile, jobs, tables, masked):
-        unit = slot - jnp.where(slot >= near, near, 0)
-        key_values, scores = [], []
-        for query_head, key_head in jobs:
-            key_value = kv_all[pl.ds(tile * blocks_per_tile, blocks_per_tile), key_head]
-            key_values.append(key_value.reshape(key_tile, LANES))
-            queries = query_buf[query_head, pl.ds(unit, count)].reshape(count * rows, LANES)
-            scores.append(
-                lax.dot_general(
-                    queries,
-                    key_values[-1],
-                    (((1,), (1,)), ((), ())),
-                    preferred_element_type=jnp.float32,
+    def visit_tiles(sections, jobs, tables):
+        for slot, count, tile, span, masked in sections:
+            unit = slot - jnp.where(slot >= near, near, 0)
+            keys = span * key_tile
+            key_values, scores = [], []
+            for query_head, key_head in jobs:
+                key_value = kv_all[pl.ds(tile * blocks_per_tile, span * blocks_per_tile), key_head]
+                key_values.append(key_value.reshape(keys, LANES))
+                queries = query_buf[query_head, pl.ds(unit, count)].reshape(count * rows, LANES)
+                scores.append(
+                    lax.dot_general(
+                        queries,
+                        key_values[-1],
+                        (((1,), (1,)), ((), ())),
+                        preferred_element_type=jnp.float32,
+                    )
                 )
+            weights = [[] for _ in jobs]
+            for first in range(0, keys, LANES):
+                columns = [[] for _ in jobs]
+                key_stamp = stamp_keys[
+                    tile + first // key_tile, :, first % key_tile : first % key_tile + LANES
+                ]
+                for top in range(0, count * rows, chunk):
+                    place, start = top // rows, top % rows
+                    query_stamp = stamp_rows[slot + place, start : start + chunk]
+                    elapsed = query_stamp - key_stamp
+                    biases = biases_of(elapsed, tables, (top // chunk + first // LANES) % 3 != 0)
+                    for score, bias, column in zip(scores, biases, columns):
+                        halved = score[top : top + chunk, first : first + LANES] + bias
+                        halved = halved.astype(jnp.bfloat16)
+                        weight = halved + halved * jnp.tanh(halved)
+                        if masked:
+                            ahead = tile * key_tile + first - block_of(slot, my_split) * rows - start
+                            weight = jnp.where(spread <= -ahead, weight.astype(jnp.float32), 0.0)
+                            weight = weight.astype(jnp.bfloat16)
+                        column.append(weight)
+                for weight, column in zip(weights, columns):
+                    weight.append(jnp.concatenate(column, axis=0))
+            for (query_head, _), weight, key_value in zip(jobs, weights, key_values):
+                sums = jnp.dot(
+                    jnp.concatenate(weight, axis=1), key_value, preferred_element_type=jnp.float32
+                )
+                total_buf[query_head, pl.ds(unit, count)] += sums.reshape(count, rows, LANES)
+
+    def visit(sections, jobs, tables):
+        def one(step, carry):
+            visit_tiles(
+                [
+                    (slot, count, group * group_tiles + span * step, span, masked)
+                    for slot, count, group, span, masked in sections
+                ],
+                jobs,
+                tables,
             )
-        weights = [[] for _ in jobs]
-        for first in range(0, key_tile, LANES):
-            columns = [[] for _ in jobs]
-            for top in range(0, count * rows, chunk):
-                place, start = top // rows, top % rows
-                query_stamp = stamp_rows[slot + place, start : start + chunk]
-                elapsed = query_stamp - stamp_keys[tile, :, first : first + LANES]
-                biases = biases_of(elapsed, tables, (top // chunk + first // LANES) % 3 != 0)
-                for score, bias, column in zip(scores, biases, columns):
-                    halved = score[top : top + chunk, first : first + LANES] + bias
-                    halved = halved.astype(jnp.bfloat16)
-                    weight = halved + halved * jnp.tanh(halved)
-                    if masked and place == 0:
-                        ahead = tile * key_tile + first - block_of(slot, my_split) * rows - start
-                        weight = jnp.where(spread <= -ahead, weight.astype(jnp.float32), 0.0)
-                        weight = weight.astype(jnp.bfloat16)
-                    column.append(weight)
-            for weight, column in zip(weights, columns):
-                weight.append(jnp.concatenate(column, axis=0))
-        for (query_head, _), weight, key_value in zip(jobs, weights, key_values):
-            sums = jnp.dot(
-                jnp.concatenate(weight, axis=1), key_value, preferred_element_type=jnp.float32
-            )
-            total_buf[query_head, pl.ds(unit, count)] += sums.reshape(count, rows, LANES)
-
-    def visit(slot, count, group, jobs, tables, masked):
+            return carry
+
         if group_tiles == 1:
-            visit_tile(slot, count, group, jobs, tables, masked)
-            return
-
-        def one(tile, carry):
-            visit_tile(slot, count, tile, jobs, tables, masked)
-            return carry
-
-        lax.fori_loop(group * group_tiles, (group + 1) * group_tiles, one, 0)
-
-    def visit_near(slot, count, group, masked):
-        visit(slot, count, group, [(0, 0), (1, 1)], near_tables, masked)
+            one(0, 0)
+        else:
+            lax.fori_loop(0, group_tiles, one, 0)
+
+    def visit_near(*pairs):
+        visit(
+            [
+                (jnp.maximum(one, other), 1, jnp.minimum(one, other), 1, masked)
+                for one, other, masked in pairs
+            ],
+            [(0, 0), (1, 1)],
+            near_tables,
+        )
 
     def back_copy(kind, unit):
         slot = unit + (near if kind == 2 else near_first)
@@ -478,7 +512,7 @@
             back_buf.at[kind, unit], target, back_sem.at[kind, unit], semaphore, block
         )
 
-    def finish(kind):
+    def finish(kind, first, count):
         def one(unit, carry):
             block, copy = back_copy(kind, unit)
             total = total_buf[kind, unit]
@@ -499,45 +533,60 @@
 
             return carry
 
-        lax.fori_loop(0, near, one, 0)
-
-    def take_near(slot, carry):
-        take_direct(slot)
-        take_query(slot)
-        return carry
-
-    lax.fori_loop(near_first, near_first + near, take_near, 0)
-
-    def near_group(group, carry):
+        lax.fori_loop(first, first + count, one, 0)
+
+    def near_at(step):
+        return near_first + lax.rem(my_place - step + near, near)
+
+    take_direct(near_at(0))
+
+    def near_step(step, carry):
+        group = near_at(step)
+
+        @pl.when(step + 1 < near)
+        def _():
+            take_direct(near_at(step + 1))
+
+        @pl.when((step + 1 == near) & (upper == 1))
+        def _():
+            for late in range(near // 2):
+                take_late_direct(near - 1 - late)
+
         take_forwarded(group)
-        rest = near_first + near - group
-
-        @pl.when(rest == 1)
-        def _():
-            visit_near(group, 1, group, True)
-
-        @pl.when(rest > 1)
-        def _():
-            visit_near(group, 2, group, True)
-
-        def two(step, inner):
-            visit_near(group + 2 + 2 * step, 2, group, False)
+        take_query(group)
+
+        @pl.when(step == 0)
+        def _():
+            visit_near((group, group, True))
+
+        @pl.when(step > 0)
+        def _():
+            visit_near((group, group, True), (group, near_at(step - 1), False))
+
+        def two(pair, inner):
+            visit_near((group, near_at(2 * pair), False), (group, near_at(2 * pair + 1), False))
             return inner
 
-        lax.fori_loop(0, (rest - 2) // 2, two, 0)
-
-        @pl.when((rest > 2) & (rest % 2 == 1))
-        def _():
-            visit_near(group + rest - 1, 1, group, False)
-
-        return carry
-
-    lax.fori_loop(near_first, near_first + near, near_group, 0)
-    finish(0)
+        lax.fori_loop(0, jnp.maximum(step - 1, 0) // 2, two, 0)
+
+        @pl.when((step > 1) & (step % 2 == 0))
+        def _():
+            visit_near((group, near_at(step - 2), False))
+
+        return carry
+
+    lax.fori_loop(0, near, near_step, 0)
+
+    @pl.when(upper == 1)
+    def _():
+        for late in range(near // 2, near):
+            take_late_direct(near - 1 - late)
+
+    finish(0, 0, near)
 
     @pl.when(upper == 0)
     def _():
-        finish(1)
+        finish(1, 0, near)
 
     lax.fori_loop(0, side, wait_far_stamps, 0)
 
@@ -546,84 +595,35 @@
         lax.fori_loop(near, 2 * near, turn_stamps, 0)
         lax.fori_loop(near, 2 * near, take_far_query, 0)
 
-    def late_at(step):
-        return lax.rem(my_place - step + near, near)
-
     @pl.when(upper == 1)
     def _():
         lax.fori_loop(0, near * group_tiles, join_stamps, 0)
-        take_late_direct(late_at(0))
+
+    halves = near // 2
 
     def square(step, carry):
-        group = late_at(step)
-
-        @pl.when(upper == 1)
-        def _():
-            take_late_forwarded(group)
-
-            @pl.when(step + 1 < near)
-            def _():
-                take_late_direct(late_at(step + 1))
-
-        visit(near, near, group, [(2 - upper, upper)], square_tables, False)
-        return carry
-
-    lax.fori_loop(0, near, square, 0)
-
-    @pl.when(upper == 0)
-    def _():
-        finish(2)
-
-    @pl.when(upper == 1)
-    def _():
-        finish(1)
-
-    def drain_both(place, target):
-        q_copy(place, target).wait_send()
-        kv_copy(place, target).wait_send()
-
-    each_near(drain_both)
-    each_far(lambda copy: copy.wait_send())
-
-    def drain(step, carry):
-        stamp_copy(lax.rem(me + step, parts)).wait_send()
-        return carry
-
-    lax.fori_loop(1, parts, drain, 0)
-
-    def drain_near(slot, carry):
-        for step in range(1, splits):
-            forward(slot, block_of(slot, my_split), step).wait_send()
-        return carry
-
-    def drain_late(slot, carry):
-        for step in range(1, splits):
-            late_forward(slot, block_of(slot, my_split), step).wait_send()
-        return carry
-
-    def drain_back(kind):
-        def one(unit, carry):
-            block, copy = back_copy(kind, unit)
-
-            @pl.when(block != me)
-            def _():
-                copy.wait_send()
-
-            return carry
-
-        lax.fori_loop(0, near, one, 0)
-
-    lax.fori_loop(near_first, near_first + near, drain_near, 0)
-    drain_back(0)
-    drain_back(1)
-
-    @pl.when(upper == 0)
-    def _():
-        drain_back(2)
-
-    @pl.when(upper == 1)
-    def _():
-        lax.fori_loop(0, near, drain_late, 0)
+        major, minor = step // halves, step % halves
+        slots = 2 * jnp.where(upper == 0, major, minor)
+        groups = 2 * (halves - 1 - jnp.where(upper == 0, minor, major))
+
+        @pl.when((upper == 1) & (minor == 0))
+        def _():
+            take_late_forwarded(groups)
+            take_late_forwarded(groups + 1)
+
+        visit([(near + slots, 2, groups, 2, False)], [(2 - upper, upper)], square_tables)
+
+        @pl.when((upper == 0) & (minor == halves - 1))
+        def _():
+            finish(2, slots, 2)
+
+        @pl.when((upper == 1) & (major == halves - 1))
+        def _():
+            finish(1, slots, 2)
+
+        return carry
+
+    lax.fori_loop(0, halves * halves, square, 0)
 
     loads[6].wait()
     loads[7].wait()
@@ -676,6 +676,53 @@
         gated.astype(jnp.bfloat16), w_out_ref[...], preferred_element_type=jnp.float32
     )
     out_ref[...] = mixed.astype(jnp.bfloat16)
+
+    def drain_both(place, target):
+        q_copy(place, target).wait_send()
+        kv_copy(place, target).wait_send()
+
+    each_near(drain_both)
+    each_far(lambda copy: copy.wait_send())
+
+    def drain(step, carry):
+        stamp_copy(lax.rem(me + step, parts)).wait_send()
+        return carry
+
+    lax.fori_loop(1, parts, drain, 0)
+
+    def drain_near(slot, carry):
+        for step in range(1, splits):
+            forward(slot, block_of(slot, my_split), step).wait_send()
+        return carry
+
+    def drain_late(slot, carry):
+        for step in range(1, splits):
+            late_forward(slot, block_of(slot, my_split), step).wait_send()
+        return carry
+
+    def drain_back(kind):
+        def one(unit, carry):
+            block, copy = back_copy(kind, unit)
+
+            @pl.when(block != me)
+            def _():
+                copy.wait_send()
+
+            return carry
+
+        lax.fori_loop(0, near, one, 0)
+
+    lax.fori_loop(near_first, near_first + near, drain_near, 0)
+    drain_back(0)
+    drain_back(1)
+
+    @pl.when(upper == 0)
+    def _():
+        drain_back(2)
+
+    @pl.when(upper == 1)
+    def _():
+        lax.fori_loop(0, near, drain_late, 0)
 
 
 def solution(mesh):
@@ -726,6 +773,7 @@
                 pltpu.SemaphoreType.DMA((3, near)),
                 pltpu.SemaphoreType.DMA((heads,)),
                 pltpu.SemaphoreType.DMA((near,)),
+                pltpu.SemaphoreType.REGULAR,
             ],
             compiler_params=pltpu.CompilerParams(
                 collective_id=0, has_side_effects=True

time: 31.4 us -> 29.7 us (0.946)
  the two profiles are of different devices: /device:TPU:25 before, /device:TPU:18 now
where the time goes in v3:
time: 29.7 us; the launch traced here: 29.6 us
  Pallas kernels  27.9 us (94%)
  local copies, waits for them, and re-layouts  1.62 us (5%)
    pallas_call x1, Pallas kernels, body(): pl.pallas_call(functools.partial(kernel, parts, heads), out_shape=jax.Sha...  27.9 us
    unnamed x1, local copies, waits for them, and re-layouts  1.62 us

profile of v3, /device:TPU:18, one launch (start us, length us, event | category | flops | bytes accessed | tf_op | source)
XLA Modules:
  0.0 29.6 jit_solution(6302436085540292875)
XLA Ops:
  0.0 27.9 %shard_map.73 = bf16[192,512]{1,0:T(8,128)(2,1)} custom-call(bf16[192,512]{1,0:T(8,128)(2,1)} %tokens_hbm.1, s32[1,192]{1,0:T(1,128)} %bitcast.5, f32[1,512]{1,0:T(1,128)} %bitcast.3, bf16[512,2048]{1,0:T(8,128)(2,1)} %w_proj_hbm.1, f32[8,16]{1,0:T(8,128)} %bias_hbm.1, f32[1,512]{1,0:T(1,128)} %bitcast.4, bf16[512,512]{1,0:T(8,128)(2,1)} %w_out_hbm.1), custom_call_target="tpu_custom_call" | custom-call | tf_op jit(solution)/shard_map/pallas_call | solution.py:738
  27.9 1.6 %copy.9 = bf16[192,512]{1,0:T(8,128)(2,1)} copy(bf16[192,512]{1,0:T(8,128)(2,1)} %shard_map.73) | data formatting | bytes 393216

commit v4 on v3

--- a/solution.py
+++ b/solution.py
@@ -51,16 +51,14 @@
     norm_gain_hbm,
     w_proj_hbm,
     bias_hbm,
-    attn_gain_hbm,
-    w_out_hbm,
-    out_ref,
+    att_out,
+    part_out,
+    gate_out,
     tokens_ref,
     stamps_ref,
     norm_gain_ref,
     w_proj_ref,
     bias_ref,
-    attn_gain_ref,
-    w_out_ref,
     kv_send,
     q_send,
     kv_all,
@@ -72,8 +70,7 @@
     total_buf,
     gate_buf,
     back_buf,
-    att_buf,
-    part_buf,
+    zero_buf,
     load_sem,
     kv_send_sem,
     q_send_sem,
@@ -87,6 +84,7 @@
     att_sem,
     part_sem,
     far_ready,
+    own_sem,
 ):
     rows, width = tokens_ref.shape
     half = rows // 2
@@ -109,8 +107,6 @@
                 (stamps_hbm, stamps_ref),
                 (bias_hbm, bias_ref),
                 (w_proj_hbm.at[:, :width], w_proj_ref.at[:, :width]),
-                (attn_gain_hbm, attn_gain_ref),
-                (w_out_hbm, w_out_ref),
             ]
         )
     ]
@@ -217,7 +213,7 @@
 
     def each_near(act):
         def one(step, carry):
-            place = lax.rem(my_place + step, near)
+            place = my_place ^ jnp.where(step == 0, 0, near - step)
             target = (near_first + place) * splits + my_home
 
             @pl.when(target != me)
@@ -232,7 +228,7 @@
         place = step + (my_place % 2) * (1 - 2 * (step % 2))
         return place + upper * (near - 1 - 2 * place)
 
-    def each_far(act):
+    def each_far(first, count, act):
         def one(step, carry):
             place = far_place(step)
             target = (far_first + place) * splits + my_home
@@ -247,7 +243,7 @@
 
             return carry
 
-        lax.fori_loop(0, near, one, 0)
+        lax.fori_loop(first, first + count, one, 0)
 
     def send_near_stamps(step, carry):
         stamp_copy(near_peer(step)).start()
@@ -278,18 +274,23 @@
         kv_all[me] = kv_send[my_place]
         q_all[my_group] = q_send[my_place]
 
+    gate_store = pltpu.make_async_copy(gate_buf, gate_out, own_sem.at[2])
+    no_part = pltpu.make_async_copy(zero_buf, part_out, own_sem.at[3])
+
     @pl.when(upper == 0)
     def _():
-        part_buf[...] = jnp.zeros_like(part_buf)
+        zero_buf[...] = jnp.zeros_like(zero_buf)
+        no_part.start()
 
     loads[5].wait()
     gate_proj = jnp.dot(normed, w_proj_ref[:, :width], preferred_element_type=jnp.float32)
     gate_buf[...] = jax.nn.silu(gate_proj).astype(jnp.bfloat16)
+    gate_store.start()
     total_buf[...] = jnp.zeros_like(total_buf)
 
     pl.semaphore_wait(far_ready, side - 1)
     lax.fori_loop(0, side, send_far_stamps, 0)
-    each_far(lambda copy: copy.start())
+    each_far(0, near // 2, lambda copy: copy.start())
 
     lane_id = lax.broadcasted_iota(jnp.int32, (8, LANES), 1)
     place_id = lax.broadcasted_iota(jnp.int32, (8, LANES), 0)
@@ -503,13 +504,18 @@
     def back_copy(kind, unit):
         slot = unit + (near if kind == 2 else near_first)
         target, semaphore = (
-            (part_buf.at[my_place], part_sem.at[my_place])
+            (part_out.at[my_place], part_sem.at[my_place])
             if kind == 2
-            else (att_buf.at[2 * my_place + kind], att_sem.at[2 * my_place + kind])
+            else (att_out.at[2 * my_place + kind], att_sem.at[2 * my_place + kind])
         )
         block = block_of(slot, my_split)
         return block, remote(
             back_buf.at[kind, unit], target, back_sem.at[kind, unit], semaphore, block
+        )
+
+    def own_copy(kind, unit):
+        return pltpu.make_async_copy(
+            back_buf.at[kind, unit], att_out.at[2 * my_place + kind], own_sem.at[kind]
         )
 
     def finish(kind, first, count):
@@ -525,7 +531,7 @@
 
             @pl.when(block == me)
             def _():
-                att_buf[2 * my_place + kind] = result
+                own_copy(kind, unit).start()
 
             @pl.when(block != me)
             def _():
@@ -536,21 +542,20 @@
         lax.fori_loop(first, first + count, one, 0)
 
     def near_at(step):
-        return near_first + lax.rem(my_place - step + near, near)
+        return near_first + (my_place ^ jnp.where(step == 0, 0, near - step))
 
     take_direct(near_at(0))
 
     def near_step(step, carry):
         group = near_at(step)
 
+        @pl.when(step == 1)
+        def _():
+            each_far(near // 2, near // 2, lambda copy: copy.start())
+
         @pl.when(step + 1 < near)
         def _():
             take_direct(near_at(step + 1))
-
-        @pl.when((step + 1 == near) & (upper == 1))
-        def _():
-            for late in range(near // 2):
-                take_late_direct(near - 1 - late)
 
         take_forwarded(group)
         take_query(group)
@@ -579,7 +584,7 @@
 
     @pl.when(upper == 1)
     def _():
-        for late in range(near // 2, near):
+        for late in range(near):
             take_late_direct(near - 1 - late)
 
     finish(0, 0, near)
@@ -625,19 +630,50 @@
 
     lax.fori_loop(0, halves * halves, square, 0)
 
-    loads[6].wait()
-    loads[7].wait()
+    def drain_both(place, target):
+        q_copy(place, target).wait_send()
+        kv_copy(place, target).wait_send()
+
+    each_near(drain_both)
+    each_far(0, near, lambda copy: copy.wait_send())
+
+    def drain(step, carry):
+        stamp_copy(lax.rem(me + step, parts)).wait_send()
+        return carry
+
+    lax.fori_loop(1, parts, drain, 0)
+
+    def drain_near(slot, carry):
+        for step in range(1, splits):
+            forward(slot, block_of(slot, my_split), step).wait_send()
+        return carry
+
+    def drain_late(slot, carry):
+        for step in range(1, splits):
+            late_forward(slot, block_of(slot, my_split), step).wait_send()
+        return carry
+
+    lax.fori_loop(near_first, near_first + near, drain_near, 0)
+
+    @pl.when(upper == 1)
+    def _():
+        lax.fori_loop(0, near, drain_late, 0)
 
     def take_back(step, carry):
         place = lax.rem(my_place + step, near)
         source = (near_first + place) * splits + my_home
 
+        @pl.when(source == me)
+        def _():
+            for head in range(2):
+                own_copy(head, 0).wait()
+
         @pl.when(source != me)
         def _():
             for head in range(2):
                 remote(
                     back_buf.at[0, 0],
-                    att_buf.at[2 * place + head],
+                    att_out.at[2 * place + head],
                     back_sem.at[0, 0],
                     att_sem.at[2 * place + head],
                     source,
@@ -647,7 +683,7 @@
         def _():
             remote(
                 back_buf.at[0, 0],
-                part_buf.at[place],
+                part_out.at[place],
                 back_sem.at[0, 0],
                 part_sem.at[place],
                 place * splits + my_home,
@@ -657,49 +693,6 @@
 
     lax.fori_loop(0, near, take_back, 0)
 
-    pieces = []
-    for pair in range(near):
-        even = att_buf[2 * pair].astype(jnp.float32) + part_buf[pair].astype(jnp.float32)
-        odd = att_buf[2 * pair + 1].astype(jnp.float32)
-        pieces.append(
-            jnp.concatenate(
-                [
-                    jnp.where(low, even, pltpu.roll(odd, head_size, 1)),
-                    jnp.where(low, pltpu.roll(even, head_size, 1), odd),
-                ],
-                axis=0,
-            )
-        )
-    attended = jnp.concatenate(pieces, axis=1)
-    gated = layer_norm(attended, attn_gain_ref[...]) * gate_buf[...].astype(jnp.float32)
-    mixed = tokens_ref[...].astype(jnp.float32) + jnp.dot(
-        gated.astype(jnp.bfloat16), w_out_ref[...], preferred_element_type=jnp.float32
-    )
-    out_ref[...] = mixed.astype(jnp.bfloat16)
-
-    def drain_both(place, target):
-        q_copy(place, target).wait_send()
-        kv_copy(place, target).wait_send()
-
-    each_near(drain_both)
-    each_far(lambda copy: copy.wait_send())
-
-    def drain(step, carry):
-        stamp_copy(lax.rem(me + step, parts)).wait_send()
-        return carry
-
-    lax.fori_loop(1, parts, drain, 0)
-
-    def drain_near(slot, carry):
-        for step in range(1, splits):
-            forward(slot, block_of(slot, my_split), step).wait_send()
-        return carry
-
-    def drain_late(slot, carry):
-        for step in range(1, splits):
-            late_forward(slot, block_of(slot, my_split), step).wait_send()
-        return carry
-
     def drain_back(kind):
         def one(unit, carry):
             block, copy = back_copy(kind, unit)
@@ -712,7 +705,6 @@
 
         lax.fori_loop(0, near, one, 0)
 
-    lax.fori_loop(near_first, near_first + near, drain_near, 0)
     drain_back(0)
     drain_back(1)
 
@@ -720,9 +712,80 @@
     def _():
         drain_back(2)
 
-    @pl.when(upper == 1)
+    gate_store.wait()
+
+    @pl.when(upper == 0)
     def _():
-        lax.fori_loop(0, near, drain_late, 0)
+        no_part.wait()
+
+
+def final_kernel(
+    att_hbm,
+    part_hbm,
+    gate_hbm,
+    tokens_hbm,
+    attn_gain_hbm,
+    w_out_hbm,
+    out_hbm,
+    att_buf,
+    part_buf,
+    gate_buf,
+    tokens_ref,
+    attn_gain_ref,
+    w_out_ref,
+    out_buf,
+    load_sem,
+    store_sem,
+):
+    loads = [
+        pltpu.make_async_copy(source, target, load_sem.at[index])
+        for index, (source, target) in enumerate(
+            [
+                (att_hbm, att_buf),
+                (part_hbm, part_buf),
+                (gate_hbm, gate_buf),
+                (attn_gain_hbm, attn_gain_ref),
+                (w_out_hbm, w_out_ref),
+                (tokens_hbm, tokens_ref),
+            ]
+        )
+    ]
+    for load in loads:
+        load.start()
+    heads, half, _ = att_buf.shape
+    head_size = tokens_ref.shape[1] // heads
+    low = lax.broadcasted_iota(jnp.int32, (1, LANES), 1) < head_size
+    for load in loads[:4]:
+        load.wait()
+    sides = []
+    for side in range(2):
+        pieces = []
+        for pair in range(heads // 2):
+            even = att_buf[2 * pair].astype(jnp.float32) + part_buf[pair].astype(jnp.float32)
+            odd = att_buf[2 * pair + 1].astype(jnp.float32)
+            if side == 0:
+                pieces.append(jnp.where(low, even, pltpu.roll(odd, head_size, 1)))
+            else:
+                pieces.append(jnp.where(low, pltpu.roll(even, head_size, 1), odd))
+        attended = jnp.concatenate(pieces, axis=1)
+        part = slice(side * half, (side + 1) * half)
+        gated = layer_norm(attended, attn_gain_ref[...]) * gate_buf[part].astype(jnp.float32)
+        sides.append(gated.astype(jnp.bfloat16))
+    loads[4].wait()
+    loads[5].wait()
+    stores = []
+    for side in range(2):
+        part = pl.ds(side * half, half)
+        mixed = tokens_ref[part].astype(jnp.float32) + jnp.dot(
+            sides[side], w_out_ref[...], preferred_element_type=jnp.float32
+        )
+        out_buf[part] = mixed.astype(jnp.bfloat16)
+        stores.append(
+            pltpu.make_async_copy(out_buf.at[part], out_hbm.at[part], store_sem.at[side])
+        )
+        stores[-1].start()
+    for store in stores:
+        store.wait()
 
 
 def solution(mesh):
@@ -734,20 +797,21 @@
         splits = parts // heads
         near = heads // 2
         blocks_per_tile = max(1, 384 // rows)
-        vmem = pl.BlockSpec(memory_space=pltpu.VMEM)
-        return pl.pallas_call(
+        att, part, gate = pl.pallas_call(
             functools.partial(kernel, parts, heads),
-            out_shape=jax.ShapeDtypeStruct((rows, width), jnp.bfloat16),
-            in_specs=[pl.BlockSpec(memory_space=pltpu.HBM)] * 7,
-            out_specs=vmem,
+            out_shape=[
+                jax.ShapeDtypeStruct((heads, rows // 2, LANES), jnp.bfloat16),
+                jax.ShapeDtypeStruct((near, rows // 2, LANES), jnp.bfloat16),
+                jax.ShapeDtypeStruct((rows, width), jnp.bfloat16),
+            ],
+            in_specs=[pl.BlockSpec(memory_space=pltpu.HBM)] * 5,
+            out_specs=[pl.BlockSpec(memory_space=pltpu.HBM)] * 3,
             scratch_shapes=[
                 pltpu.VMEM((rows, width), jnp.bfloat16),
                 pltpu.VMEM((1, rows), jnp.int32),
                 pltpu.VMEM((1, width), jnp.float32),
                 pltpu.VMEM(w_proj.shape, jnp.bfloat16),
                 pltpu.SMEM(rel_bias.shape, jnp.float32),
-                pltpu.VMEM((1, width), jnp.float32),
-                pltpu.VMEM(w_out.shape, jnp.bfloat16),
                 pltpu.VMEM((near, 2, rows, LANES), jnp.bfloat16),
                 pltpu.VMEM((near, 2, rows // 2, LANES), jnp.bfloat16),
                 pltpu.VMEM((parts, 2, rows, LANES), jnp.bfloat16),
@@ -759,9 +823,8 @@
                 pltpu.VMEM((3, near, rows, LANES), jnp.float32),
                 pltpu.VMEM((rows, width), jnp.bfloat16),
                 pltpu.VMEM((3, near, rows // 2, LANES), jnp.bfloat16),
-                pltpu.VMEM((heads, rows // 2, LANES), jnp.bfloat16),
                 pltpu.VMEM((near, rows // 2, LANES), jnp.bfloat16),
-                pltpu.SemaphoreType.DMA((8,)),
+                pltpu.SemaphoreType.DMA((6,)),
                 pltpu.SemaphoreType.DMA((near,)),
                 pltpu.SemaphoreType.DMA((near,)),
                 pltpu.SemaphoreType.DMA((near,)),
@@ -774,6 +837,7 @@
                 pltpu.SemaphoreType.DMA((heads,)),
                 pltpu.SemaphoreType.DMA((near,)),
                 pltpu.SemaphoreType.REGULAR,
+                pltpu.SemaphoreType.DMA((4,)),
             ],
             compiler_params=pltpu.CompilerParams(
                 collective_id=0, has_side_effects=True
@@ -784,9 +848,25 @@
             norm_gain.reshape(1, width),
             w_proj,
             rel_bias,
-            attn_gain.reshape(1, width),
-            w_out,
-        )
+        )
+        hbm = pl.BlockSpec(memory_space=pltpu.HBM)
+        return pl.pallas_call(
+            final_kernel,
+            out_shape=jax.ShapeDtypeStruct((rows, width), jnp.bfloat16),
+            in_specs=[hbm] * 6,
+            out_specs=hbm,
+            scratch_shapes=[
+                pltpu.VMEM((heads, rows // 2, LANES), jnp.bfloat16),
+                pltpu.VMEM((near, rows // 2, LANES), jnp.bfloat16),
+                pltpu.VMEM((rows, width), jnp.bfloat16),
+                pltpu.VMEM((rows, width), jnp.bfloat16),
+                pltpu.VMEM((1, width), jnp.float32),
+                pltpu.VMEM(w_out.shape, jnp.bfloat16),
+                pltpu.VMEM((rows, width), jnp.bfloat16),
+                pltpu.SemaphoreType.DMA((6,)),
+                pltpu.SemaphoreType.DMA((2,)),
+            ],
+        )(att, part, gate, tokens, attn_gain.reshape(1, width), w_out)
 
     return jax.shard_map(
         body,

time: 29.7 us -> 28.1 us (0.946); the launches traced: 29.6 us -> 27.5 us
  local copies, waits for them, and re-layouts: 1.62 us -> 0 us
  Pallas kernels: 27.9 us -> 27.5 us
    unnamed x1 -> x0, local copies, waits for them, and re-layouts: 1.62 us -> none
    pallas_call x1 -> x2, Pallas kernels: 27.9 us -> 27.5 us  [the longest x1 25.1 us: body(): pl.pallas_call(functools.partial(kernel, parts, heads), out_shape=[jax.Sh...]
where the time goes in v4:
time: 28.1 us; the launch traced here: 27.5 us
  Pallas kernels  27.5 us (98%)
    pallas_call x1, Pallas kernels, body(): pl.pallas_call(functools.partial(kernel, parts, heads), out_shape=[jax.Sh...  25.1 us
    pallas_call x1, Pallas kernels, body(): pl.pallas_call(final_kernel, out_shape=jax.ShapeDtypeStruct((rows, width)...  2.44 us

profile of v4, /device:TPU:18, one launch (start us, length us, event | category | flops | bytes accessed | tf_op | source)
XLA Modules:
  0.0 27.5 jit_solution(4864795589927840210)
XLA Ops:
  0.0 25.1 %shard_map.73 = (bf16[8,96,128]{2,1,0:T(8,128)(2,1)}, bf16[4,96,128]{2,1,0:T(8,128)(2,1)}, bf16[192,512]{1,0:T(8,128)(2,1)}) custom-call(bf16[192,512]{1,0:T(8,128)(2,1)} %tokens_hbm.3, s32[1,192]{1,0:T(1,128)} %bitcast.5, f32[1,512]{1,0:T(1,128)} %bitcast.3, bf16[512,2048]{1,0:T(8,128)(2,1)} %w_proj_hbm.1, f32[8,16]{1,0:T(8,128)} %bias_hbm.1), custom_call_target="tpu_custom_call" | custom-call | tf_op jit(solution)/shard_map/pallas_call | solution.py:800
  25.1 2.4 %shard_map.74 = bf16[192,512]{1,0:T(8,128)(2,1)} custom-call(bf16[8,96,128]{2,1,0:T(8,128)(2,1)} %get-tuple-element.8.att_hbm, bf16[4,96,128]{2,1,0:T(8,128)(2,1)} %get-tuple-element.9.part_hbm, bf16[192,512]{1,0:T(8,128)(2,1)} %get-tuple-element.10.gate_hbm, bf16[192,512]{1,0:T(8,128)(2,1)} %tokens_hbm.3, f32[1,512]{1,0:T(1,128)} %bitcast.4, ...), custom_call_target="tpu_custom_call" | custom-call | tf_op jit(solution)/shard_map/pallas_call | solution.py:853

commit v5 on v4

--- a/solution.py
+++ b/solution.py
@@ -78,6 +78,7 @@
     fwd_sem,
     kv_sem,
     q_sem,
+    far_q_sem,
     stamp_send_sem,
     stamp_sem,
     back_sem,
@@ -188,27 +189,31 @@
 
     my_home = split_of(me)
 
-    def stamp_copy(target):
+    def stamp_copy(target, kind):
         return remote(
-            stamps_ref, stamp_all.at[me], stamp_send_sem.at[target], stamp_sem.at[me], target
-        )
+            stamps_ref, stamp_all.at[me], stamp_send_sem.at[kind], stamp_sem.at[kind], target
+        )
+
+    def all_stamps(kind):
+        some = stamp_all.at[pl.ds(0, side - 1 + kind)]
+        return remote(some, some, stamp_send_sem.at[kind], stamp_sem.at[kind], near_peer(1))
 
     def kv_copy(place, target):
-        return remote(kv_send.at[place], kv_all.at[me], kv_send_sem.at[place], kv_sem.at[me], target)
+        return remote(kv_send.at[place], kv_all.at[me], kv_send_sem, kv_sem.at[me], target)
 
     def q_copy(place, target):
         return remote(
-            q_send.at[place], q_all.at[my_group], q_send_sem.at[place], q_sem.at[my_group], target
+            q_send.at[place], q_all.at[my_group], q_send_sem, q_sem.at[my_place], target
         )
 
     def late_kv_copy(place, target):
         return remote(
-            kv_send.at[place, 1], kv_all.at[me, 1], far_send_sem.at[place], kv_sem.at[me], target
+            kv_send.at[place, 1], kv_all.at[me, 1], far_send_sem, kv_sem.at[me], target
         )
 
     def early_q_copy(place, target):
         return remote(
-            q_send.at[place, 0], q_all.at[my_group, 0], far_send_sem.at[place], q_sem.at[my_group], target
+            q_send.at[place, 0], q_all.at[my_group, 0], far_send_sem, far_q_sem, target
         )
 
     def each_near(act):
@@ -246,11 +251,11 @@
         lax.fori_loop(first, first + count, one, 0)
 
     def send_near_stamps(step, carry):
-        stamp_copy(near_peer(step)).start()
+        stamp_copy(near_peer(step), 0).start()
         return carry
 
     def send_far_stamps(step, carry):
-        stamp_copy(far_peer(step)).start()
+        stamp_copy(far_peer(step), 1).start()
         return carry
 
     def start_both(place, target):
@@ -328,19 +333,6 @@
             )
         return biases
 
-    def wait_stamps(source):
-        remote(
-            stamps_ref, stamp_all.at[source], stamp_send_sem.at[source], stamp_sem.at[source], source
-        ).wait_recv()
-
-    def wait_near_stamps(step, carry):
-        wait_stamps(near_peer(step))
-        return carry
-
-    def wait_far_stamps(step, carry):
-        wait_stamps(far_peer(step))
-        return carry
-
     def join_stamps(tile, carry):
         stamp_keys[tile] = jnp.concatenate(
             [stamp_all[tile * blocks_per_tile + place] for place in range(blocks_per_tile)], axis=1
@@ -352,20 +344,20 @@
         stamp_rows[slot] = jnp.transpose(jnp.broadcast_to(stamp_all[block], (LANES, rows)))
         return carry
 
-    lax.fori_loop(1, side, wait_near_stamps, 0)
+    all_stamps(0).wait_recv()
     lax.fori_loop(near_first * group_tiles, (near_first + near) * group_tiles, join_stamps, 0)
     lax.fori_loop(near_first, near_first + near, turn_stamps, 0)
 
-    def forward(slot, source, step):
+    def forward(source, step):
         peer = my_group * splits + lax.rem(my_split + step, splits)
         return remote(
-            kv_all.at[source], kv_all.at[source], fwd_sem.at[slot, step], kv_sem.at[source], peer
-        )
-
-    def late_forward(slot, source, step):
+            kv_all.at[source], kv_all.at[source], fwd_sem.at[0], kv_sem.at[source], peer
+        )
+
+    def late_forward(source, step):
         peer = my_group * splits + lax.rem(my_split + step, splits)
         return remote(
-            kv_all.at[source, 1], kv_all.at[source, 1], fwd_sem.at[slot, step], kv_sem.at[source], peer
+            kv_all.at[source, 1], kv_all.at[source, 1], fwd_sem.at[1], kv_sem.at[source], peer
         )
 
     def take_direct(slot):
@@ -374,29 +366,29 @@
         @pl.when(source != me)
         def _():
             remote(
-                kv_send.at[0], kv_all.at[source], kv_send_sem.at[0], kv_sem.at[source], source
+                kv_send.at[0], kv_all.at[source], kv_send_sem, kv_sem.at[source], source
             ).wait_recv()
 
         for step in range(1, splits):
-            forward(slot, source, step).start()
+            forward(source, step).start()
 
     def take_forwarded(slot):
         for step in range(1, splits):
             source = block_of(slot, lax.rem(my_split + step, splits))
-            forward(slot, source, step).wait_recv()
+            forward(source, step).wait_recv()
 
     def take_late_direct(slot):
         source = block_of(slot, my_split)
         remote(
-            kv_send.at[0, 1], kv_all.at[source, 1], far_send_sem.at[0], kv_sem.at[source], source
+            kv_send.at[0, 1], kv_all.at[source, 1], far_send_sem, kv_sem.at[source], source
         ).wait_recv()
         for step in range(1, splits):
-            late_forward(slot, source, step).start()
+            late_forward(source, step).start()
 
     def take_late_forwarded(slot):
         for step in range(1, splits):
             source = block_of(slot, lax.rem(my_split + step, splits))
-            late_forward(slot, source, step).wait_recv()
+            late_forward(source, step).wait_recv()
 
     def unpack(packed):
         packed = packed.astype(jnp.float32)
@@ -410,19 +402,19 @@
         @pl.when(source != me)
         def _():
             remote(
-                q_send.at[0], q_all.at[slot], q_send_sem.at[0], q_sem.at[slot], source
+                q_send.at[0], q_all.at[slot], q_send_sem, q_sem.at[slot - near_first], source
             ).wait_recv()
 
         for head in range(2):
             query_buf[head, slot - near_first] = unpack(q_all[slot, head])
 
     def take_far_query(slot, carry):
-        source = block_of(slot, my_split)
-        remote(
-            q_send.at[0, 0], q_all.at[slot, 0], far_send_sem.at[0], q_sem.at[slot], source
-        ).wait_recv()
         query_buf[2, slot - near] = unpack(q_all[slot, 0])
         return carry
+
+    def all_far_queries():
+        some = q_all.at[pl.ds(0, near), 0]
+        return remote(some, some, far_send_sem, far_q_sem, near_peer(1))
 
     chunk = 64
     row_id = lax.broadcasted_iota(jnp.int32, (chunk, LANES), 0)
@@ -504,13 +496,13 @@
     def back_copy(kind, unit):
         slot = unit + (near if kind == 2 else near_first)
         target, semaphore = (
-            (part_out.at[my_place], part_sem.at[my_place])
+            (part_out.at[my_place], part_sem)
             if kind == 2
-            else (att_out.at[2 * my_place + kind], att_sem.at[2 * my_place + kind])
+            else (att_out.at[2 * my_place + kind], att_sem)
         )
         block = block_of(slot, my_split)
         return block, remote(
-            back_buf.at[kind, unit], target, back_sem.at[kind, unit], semaphore, block
+            back_buf.at[kind, unit], target, back_sem.at[kind], semaphore, block
         )
 
     def own_copy(kind, unit):
@@ -593,11 +585,12 @@
     def _():
         finish(1, 0, near)
 
-    lax.fori_loop(0, side, wait_far_stamps, 0)
+    all_stamps(1).wait_recv()
 
     @pl.when(upper == 0)
     def _():
         lax.fori_loop(near, 2 * near, turn_stamps, 0)
+        all_far_queries().wait_recv()
         lax.fori_loop(near, 2 * near, take_far_query, 0)
 
     @pl.when(upper == 1)
@@ -630,93 +623,59 @@
 
     lax.fori_loop(0, halves * halves, square, 0)
 
-    def drain_both(place, target):
-        q_copy(place, target).wait_send()
-        kv_copy(place, target).wait_send()
-
-    each_near(drain_both)
-    each_far(0, near, lambda copy: copy.wait_send())
-
-    def drain(step, carry):
-        stamp_copy(lax.rem(me + step, parts)).wait_send()
-        return carry
-
-    lax.fori_loop(1, parts, drain, 0)
-
-    def drain_near(slot, carry):
-        for step in range(1, splits):
-            forward(slot, block_of(slot, my_split), step).wait_send()
-        return carry
-
-    def drain_late(slot, carry):
-        for step in range(1, splits):
-            late_forward(slot, block_of(slot, my_split), step).wait_send()
-        return carry
-
-    lax.fori_loop(near_first, near_first + near, drain_near, 0)
+    all_stamps(0).wait_send()
+    all_stamps(1).wait_send()
+
+    def forwards():
+        some = kv_all.at[pl.ds(0, near * (splits - 1))]
+        return remote(some, some, fwd_sem.at[0], fwd_sem.at[0], near_peer(1))
+
+    def late_forwards():
+        some = kv_all.at[pl.ds(0, near * (splits - 1)), 1]
+        return remote(some, some, fwd_sem.at[1], fwd_sem.at[1], near_peer(1))
+
+    def wait_near(count):
+        some = kv_all.at[pl.ds(0, count)]
+        remote(some, some, kv_send_sem, kv_send_sem, near_peer(1)).wait_send()
+        some = q_all.at[pl.ds(0, count)]
+        remote(some, some, q_send_sem, q_send_sem, near_peer(1)).wait_send()
+
+    def results(count, send, receive):
+        some = att_out.at[pl.ds(0, count)]
+        return remote(some, some, send, receive, near_peer(1))
+
+    home = my_home == my_split
+    forwards().wait_send()
+
+    @pl.when(home)
+    def _():
+        wait_near(near - 1)
+        results(2 * near - 2, att_sem, att_sem).wait_recv()
+        for kind in range(2):
+            own_copy(kind, 0).wait()
+            results(near - 1, back_sem.at[kind], back_sem.at[kind]).wait_send()
+
+    @pl.when(jnp.logical_not(home))
+    def _():
+        wait_near(near)
+        results(2 * near, att_sem, att_sem).wait_recv()
+        for kind in range(2):
+            results(near, back_sem.at[kind], back_sem.at[kind]).wait_send()
+
+    @pl.when(upper == 0)
+    def _():
+        some = kv_send.at[:, 1]
+        remote(some, some, far_send_sem, far_send_sem, near_peer(1)).wait_send()
+        results(near, back_sem.at[2], back_sem.at[2]).wait_send()
+        no_part.wait()
 
     @pl.when(upper == 1)
     def _():
-        lax.fori_loop(0, near, drain_late, 0)
-
-    def take_back(step, carry):
-        place = lax.rem(my_place + step, near)
-        source = (near_first + place) * splits + my_home
-
-        @pl.when(source == me)
-        def _():
-            for head in range(2):
-                own_copy(head, 0).wait()
-
-        @pl.when(source != me)
-        def _():
-            for head in range(2):
-                remote(
-                    back_buf.at[0, 0],
-                    att_out.at[2 * place + head],
-                    back_sem.at[0, 0],
-                    att_sem.at[2 * place + head],
-                    source,
-                ).wait_recv()
-
-        @pl.when(upper == 1)
-        def _():
-            remote(
-                back_buf.at[0, 0],
-                part_out.at[place],
-                back_sem.at[0, 0],
-                part_sem.at[place],
-                place * splits + my_home,
-            ).wait_recv()
-
-        return carry
-
-    lax.fori_loop(0, near, take_back, 0)
-
-    def drain_back(kind):
-        def one(unit, carry):
-            block, copy = back_copy(kind, unit)
-
-            @pl.when(block != me)
-            def _():
-                copy.wait_send()
-
-            return carry
-
-        lax.fori_loop(0, near, one, 0)
-
-    drain_back(0)
-    drain_back(1)
-
-    @pl.when(upper == 0)
-    def _():
-        drain_back(2)
+        all_far_queries().wait_send()
+        late_forwards().wait_send()
+        results(near, part_sem, part_sem).wait_recv()
 
     gate_store.wait()
-
-    @pl.when(upper == 0)
-    def _():
-        no_part.wait()
 
 
 def final_kernel(
@@ -825,17 +784,18 @@
                 pltpu.VMEM((3, near, rows // 2, LANES), jnp.bfloat16),
                 pltpu.VMEM((near, rows // 2, LANES), jnp.bfloat16),
                 pltpu.SemaphoreType.DMA((6,)),
+                pltpu.SemaphoreType.DMA,
+                pltpu.SemaphoreType.DMA,
+                pltpu.SemaphoreType.DMA,
+                pltpu.SemaphoreType.DMA((2,)),
+                pltpu.SemaphoreType.DMA((parts,)),
                 pltpu.SemaphoreType.DMA((near,)),
-                pltpu.SemaphoreType.DMA((near,)),
-                pltpu.SemaphoreType.DMA((near,)),
-                pltpu.SemaphoreType.DMA((heads, splits)),
-                pltpu.SemaphoreType.DMA((parts,)),
-                pltpu.SemaphoreType.DMA((heads,)),
-                pltpu.SemaphoreType.DMA((parts,)),
-                pltpu.SemaphoreType.DMA((parts,)),
-                pltpu.SemaphoreType.DMA((3, near)),
-                pltpu.SemaphoreType.DMA((heads,)),
-                pltpu.SemaphoreType.DMA((near,)),
+                pltpu.SemaphoreType.DMA,
+                pltpu.SemaphoreType.DMA((2,)),
+                pltpu.SemaphoreType.DMA((2,)),
+                pltpu.SemaphoreType.DMA((3,)),
+                pltpu.SemaphoreType.DMA,
+                pltpu.SemaphoreType.DMA,
                 pltpu.SemaphoreType.REGULAR,
                 pltpu.SemaphoreType.DMA((4,)),
             ],

time: 28.1 us -> 27.4 us (0.975)
  Pallas kernels: 27.5 us -> 26.9 us
    pallas_call x1, Pallas kernels: 25.1 us -> 24.4 us  [body(): pl.pallas_call(functools.partial(kernel, parts, heads), out_shape=[jax.Sh...]
where the time goes in v5:
time: 27.4 us; the launch traced here: 26.9 us
  Pallas kernels  26.9 us (98%)
    pallas_call x1, Pallas kernels, body(): pl.pallas_call(functools.partial(kernel, parts, heads), out_shape=[jax.Sh...  24.4 us
    pallas_call x1, Pallas kernels, body(): pl.pallas_call(final_kernel, out_shape=jax.ShapeDtypeStruct((rows, width)...  2.45 us

profile of v5, /device:TPU:18, one launch (start us, length us, event | category | flops | bytes accessed | tf_op | source)
XLA Modules:
  0.0 26.9 jit_solution(16856246108996681999)
XLA Ops:
  0.0 24.4 %shard_map.73 = (bf16[8,96,128]{2,1,0:T(8,128)(2,1)}, bf16[4,96,128]{2,1,0:T(8,128)(2,1)}, bf16[192,512]{1,0:T(8,128)(2,1)}) custom-call(bf16[192,512]{1,0:T(8,128)(2,1)} %tokens_hbm.3, s32[1,192]{1,0:T(1,128)} %bitcast.5, f32[1,512]{1,0:T(1,128)} %bitcast.3, bf16[512,2048]{1,0:T(8,128)(2,1)} %w_proj_hbm.1, f32[8,16]{1,0:T(8,128)} %bias_hbm.1), custom_call_target="tpu_custom_call" | custom-call | tf_op jit(solution)/shard_map/pallas_call | solution.py:759
  24.4 2.4 %shard_map.74 = bf16[192,512]{1,0:T(8,128)(2,1)} custom-call(bf16[8,96,128]{2,1,0:T(8,128)(2,1)} %get-tuple-element.8.att_hbm, bf16[4,96,128]{2,1,0:T(8,128)(2,1)} %get-tuple-element.9.part_hbm, bf16[192,512]{1,0:T(8,128)(2,1)} %get-tuple-element.10.gate_hbm, bf16[192,512]{1,0:T(8,128)(2,1)} %tokens_hbm.3, f32[1,512]{1,0:T(1,128)} %bitcast.4, ...), custom_call_target="tpu_custom_call" | custom-call | tf_op jit(solution)/shard_map/pallas_call | solution.py:813

commit v6 on v5

--- a/solution.py
+++ b/solution.py
@@ -229,6 +229,9 @@
 
         lax.fori_loop(0, near, one, 0)
 
+    relays = (1 - upper) * (my_place // (near // 2)) * (near // 2)
+    farther = jnp.maximum(relays, upper * (near // 2))
+
     def far_place(step):
         place = step + (my_place % 2) * (1 - 2 * (step % 2))
         return place + upper * (near - 1 - 2 * place)
@@ -360,6 +363,15 @@
             kv_all.at[source, 1], kv_all.at[source, 1], fwd_sem.at[1], kv_sem.at[source], peer
         )
 
+    def relay(source):
+        return remote(
+            kv_all.at[source, 1],
+            kv_all.at[source, 1],
+            fwd_sem.at[1],
+            kv_sem.at[source],
+            (far_first + my_place) * splits + my_split,
+        )
+
     def take_direct(slot):
         source = block_of(slot, my_split)
 
@@ -371,6 +383,10 @@
 
         for step in range(1, splits):
             forward(source, step).start()
+
+        @pl.when(slot < relays)
+        def _():
+            relay(source).start()
 
     def take_forwarded(slot):
         for step in range(1, splits):
@@ -541,9 +557,9 @@
     def near_step(step, carry):
         group = near_at(step)
 
-        @pl.when(step == 1)
-        def _():
-            each_far(near // 2, near // 2, lambda copy: copy.start())
+        @pl.when((step == 1) & (farther > 0))
+        def _():
+            each_far(near // 2, farther, lambda copy: copy.start())
 
         @pl.when(step + 1 < near)
         def _():
@@ -551,6 +567,11 @@
 
         take_forwarded(group)
         take_query(group)
+
+        @pl.when((upper == 1) & (step + 1 == near))
+        def _():
+            for late in range(near // 2, near):
+                take_late_direct(late)
 
         @pl.when(step == 0)
         def _():
@@ -574,34 +595,28 @@
 
     lax.fori_loop(0, near, near_step, 0)
 
-    @pl.when(upper == 1)
-    def _():
-        for late in range(near):
-            take_late_direct(near - 1 - late)
-
-    finish(0, 0, near)
-
     @pl.when(upper == 0)
     def _():
+        finish(0, 0, near)
         finish(1, 0, near)
-
-    all_stamps(1).wait_recv()
-
-    @pl.when(upper == 0)
-    def _():
+        all_stamps(1).wait_recv()
         lax.fori_loop(near, 2 * near, turn_stamps, 0)
         all_far_queries().wait_recv()
         lax.fori_loop(near, 2 * near, take_far_query, 0)
 
     @pl.when(upper == 1)
     def _():
+        for late in range(near // 2):
+            take_late_direct(late)
+        finish(0, 0, near)
+        all_stamps(1).wait_recv()
         lax.fori_loop(0, near * group_tiles, join_stamps, 0)
 
     halves = near // 2
 
     def square(step, carry):
         major, minor = step // halves, step % halves
-        slots = 2 * jnp.where(upper == 0, major, minor)
+        slots = 2 * jnp.where(upper == 0, halves - 1 - major, minor)
         groups = 2 * (halves - 1 - jnp.where(upper == 0, minor, major))
 
         @pl.when((upper == 1) & (minor == 0))
@@ -664,8 +679,17 @@
 
     @pl.when(upper == 0)
     def _():
-        some = kv_send.at[:, 1]
-        remote(some, some, far_send_sem, far_send_sem, near_peer(1)).wait_send()
+        def wait_late(count, semaphore):
+            some = kv_send.at[pl.ds(0, count), 1]
+            remote(some, some, semaphore, semaphore, near_peer(1)).wait_send()
+
+        wait_late(near // 2, far_send_sem)
+
+        @pl.when(relays > 0)
+        def _():
+            wait_late(near // 2, far_send_sem)
+            wait_late(near // 2, fwd_sem.at[1])
+
         results(near, back_sem.at[2], back_sem.at[2]).wait_send()
         no_part.wait()
 
@@ -716,7 +740,7 @@
     low = lax.broadcasted_iota(jnp.int32, (1, LANES), 1) < head_size
     for load in loads[:4]:
         load.wait()
-    sides = []
+    stores = []
     for side in range(2):
         pieces = []
         for pair in range(heads // 2):
@@ -729,18 +753,16 @@
         attended = jnp.concatenate(pieces, axis=1)
         part = slice(side * half, (side + 1) * half)
         gated = layer_norm(attended, attn_gain_ref[...]) * gate_buf[part].astype(jnp.float32)
-        sides.append(gated.astype(jnp.bfloat16))
-    loads[4].wait()
-    loads[5].wait()
-    stores = []
-    for side in range(2):
-        part = pl.ds(side * half, half)
+        if side == 0:
+            loads[4].wait()
+            loads[5].wait()
         mixed = tokens_ref[part].astype(jnp.float32) + jnp.dot(
-            sides[side], w_out_ref[...], preferred_element_type=jnp.float32
+            gated.astype(jnp.bfloat16), w_out_ref[...], preferred_element_type=jnp.float32
         )
         out_buf[part] = mixed.astype(jnp.bfloat16)
+        rows = pl.ds(side * half, half)
         stores.append(
-            pltpu.make_async_copy(out_buf.at[part], out_hbm.at[part], store_sem.at[side])
+            pltpu.make_async_copy(out_buf.at[rows], out_hbm.at[rows], store_sem.at[side])
         )
         stores[-1].start()
     for store in stores:

time: 27.4 us -> 26.9 us (0.982); the launches traced: 26.9 us -> 26.7 us
  no operation moved by 1% of the time
where the time goes in v6:
time: 26.9 us; the launch traced here: 26.7 us
  Pallas kernels  26.7 us (99%)
    pallas_call x1, Pallas kernels, body(): pl.pallas_call(functools.partial(kernel, parts, heads), out_shape=[jax.Sh...  24.2 us
    pallas_call x1, Pallas kernels, body(): pl.pallas_call(final_kernel, out_shape=jax.ShapeDtypeStruct((rows, width)...  2.52 us

profile of v6, /device:TPU:18, one launch (start us, length us, event | category | flops | bytes accessed | tf_op | source)
XLA Modules:
  0.0 26.7 jit_solution(12240312073712800706)
XLA Ops:
  0.0 24.2 %shard_map.73 = (bf16[8,96,128]{2,1,0:T(8,128)(2,1)}, bf16[4,96,128]{2,1,0:T(8,128)(2,1)}, bf16[192,512]{1,0:T(8,128)(2,1)}) custom-call(bf16[192,512]{1,0:T(8,128)(2,1)} %tokens_hbm.3, s32[1,192]{1,0:T(1,128)} %bitcast.5, f32[1,512]{1,0:T(1,128)} %bitcast.3, bf16[512,2048]{1,0:T(8,128)(2,1)} %w_proj_hbm.1, f32[8,16]{1,0:T(8,128)} %bias_hbm.1), custom_call_target="tpu_custom_call" | custom-call | tf_op jit(solution)/shard_map/pallas_call | solution.py:781
  24.2 2.5 %shard_map.74 = bf16[192,512]{1,0:T(8,128)(2,1)} custom-call(bf16[8,96,128]{2,1,0:T(8,128)(2,1)} %get-tuple-element.8.att_hbm, bf16[4,96,128]{2,1,0:T(8,128)(2,1)} %get-tuple-element.9.part_hbm, bf16[192,512]{1,0:T(8,128)(2,1)} %get-tuple-element.10.gate_hbm, bf16[192,512]{1,0:T(8,128)(2,1)} %tokens_hbm.3, f32[1,512]{1,0:T(1,128)} %bitcast.4, ...), custom_call_target="tpu_custom_call" | custom-call | tf_op jit(solution)/shard_map/pallas_call | solution.py:835

commit v7 on v6

--- a/solution.py
+++ b/solution.py
@@ -218,7 +218,7 @@
 
     def each_near(act):
         def one(step, carry):
-            place = my_place ^ jnp.where(step == 0, 0, near - step)
+            place = my_place ^ step
             target = (near_first + place) * splits + my_home
 
             @pl.when(target != me)
@@ -467,13 +467,11 @@
                     biases = biases_of(elapsed, tables, (top // chunk + first // LANES) % 3 != 0)
                     for score, bias, column in zip(scores, biases, columns):
                         halved = score[top : top + chunk, first : first + LANES] + bias
-                        halved = halved.astype(jnp.bfloat16)
                         weight = halved + halved * jnp.tanh(halved)
                         if masked:
                             ahead = tile * key_tile + first - block_of(slot, my_split) * rows - start
-                            weight = jnp.where(spread <= -ahead, weight.astype(jnp.float32), 0.0)
-                            weight = weight.astype(jnp.bfloat16)
-                        column.append(weight)
+                            weight = jnp.where(spread <= -ahead, weight, 0.0)
+                        column.append(weight.astype(jnp.bfloat16))
                 for weight, column in zip(weights, columns):
                     weight.append(jnp.concatenate(column, axis=0))
             for (query_head, _), weight, key_value in zip(jobs, weights, key_values):
@@ -550,7 +548,7 @@
         lax.fori_loop(first, first + count, one, 0)
 
     def near_at(step):
-        return near_first + (my_place ^ jnp.where(step == 0, 0, near - step))
+        return near_first + (my_place ^ step)
 
     take_direct(near_at(0))
 

time: 26.9 us -> 27 us (level); the launches traced: 26.7 us -> 26.5 us
    pallas_call x1, Pallas kernels: 24.2 us -> 23.9 us  [body(): pl.pallas_call(functools.partial(kernel, parts, heads), out_shape=[jax.Sh...]
where the time goes in v7:
time: 27 us; the launch traced here: 26.5 us
  Pallas kernels  26.5 us (98%)
    pallas_call x1, Pallas kernels, body(): pl.pallas_call(functools.partial(kernel, parts, heads), out_shape=[jax.Sh...  23.9 us
    pallas_call x1, Pallas kernels, body(): pl.pallas_call(final_kernel, out_shape=jax.ShapeDtypeStruct((rows, width)...  2.52 us

profile of v7, /device:TPU:18, one launch (start us, length us, event | category | flops | bytes accessed | tf_op | source)
XLA Modules:
  0.0 26.5 jit_solution(4829336767814867852)
XLA Ops:
  0.0 23.9 %shard_map.73 = (bf16[8,96,128]{2,1,0:T(8,128)(2,1)}, bf16[4,96,128]{2,1,0:T(8,128)(2,1)}, bf16[192,512]{1,0:T(8,128)(2,1)}) custom-call(bf16[192,512]{1,0:T(8,128)(2,1)} %tokens_hbm.3, s32[1,192]{1,0:T(1,128)} %bitcast.5, f32[1,512]{1,0:T(1,128)} %bitcast.3, bf16[512,2048]{1,0:T(8,128)(2,1)} %w_proj_hbm.1, f32[8,16]{1,0:T(8,128)} %bias_hbm.1), custom_call_target="tpu_custom_call" | custom-call | tf_op jit(solution)/shard_map/pallas_call | solution.py:779
  23.9 2.5 %shard_map.74 = bf16[192,512]{1,0:T(8,128)(2,1)} custom-call(bf16[8,96,128]{2,1,0:T(8,128)(2,1)} %get-tuple-element.8.att_hbm, bf16[4,96,128]{2,1,0:T(8,128)(2,1)} %get-tuple-element.9.part_hbm, bf16[192,512]{1,0:T(8,128)(2,1)} %get-tuple-element.10.gate_hbm, bf16[192,512]{1,0:T(8,128)(2,1)} %tokens_hbm.3, f32[1,512]{1,0:T(1,128)} %bitcast.4, ...), custom_call_target="tpu_custom_call" | custom-call | tf_op jit(solution)/shard_map/pallas_call | solution.py:833

commit v8 on v7

--- a/solution.py
+++ b/solution.py
@@ -524,24 +524,28 @@
             back_buf.at[kind, unit], att_out.at[2 * my_place + kind], own_sem.at[kind]
         )
 
-    def finish(kind, first, count):
+    def finish(kinds, first, count):
         def one(unit, carry):
-            block, copy = back_copy(kind, unit)
-            total = total_buf[kind, unit]
-            result = jnp.where(low, pltpu.roll(total[:half], head_size, 1), total[half:])
-            result = result.astype(jnp.bfloat16)
-            back_buf[kind, unit] = result
-            if kind == 2:
-                copy.start()
-                return carry
-
-            @pl.when(block == me)
-            def _():
-                own_copy(kind, unit).start()
-
-            @pl.when(block != me)
-            def _():
-                copy.start()
+            results = []
+            for kind in kinds:
+                total = total_buf[kind, unit]
+                result = jnp.where(low, pltpu.roll(total[:half], head_size, 1), total[half:])
+                results.append(result.astype(jnp.bfloat16))
+            for kind, result in zip(kinds, results):
+                back_buf[kind, unit] = result
+            for kind in kinds:
+                block, copy = back_copy(kind, unit)
+                if kind == 2:
+                    copy.start()
+                    continue
+
+                @pl.when(block == me)
+                def _(kind=kind):
+                    own_copy(kind, unit).start()
+
+                @pl.when(block != me)
+                def _(copy=copy):
+                    copy.start()
 
             return carry
 
@@ -595,8 +599,7 @@
 
     @pl.when(upper == 0)
     def _():
-        finish(0, 0, near)
-        finish(1, 0, near)
+        finish((0, 1), 0, near)
         all_stamps(1).wait_recv()
         lax.fori_loop(near, 2 * near, turn_stamps, 0)
         all_far_queries().wait_recv()
@@ -606,7 +609,7 @@
     def _():
         for late in range(near // 2):
             take_late_direct(late)
-        finish(0, 0, near)
+        finish((0,), 0, near)
         all_stamps(1).wait_recv()
         lax.fori_loop(0, near * group_tiles, join_stamps, 0)
 
@@ -626,11 +629,11 @@
 
         @pl.when((upper == 0) & (minor == halves - 1))
         def _():
-            finish(2, slots, 2)
+            finish((2,), slots, 2)
 
         @pl.when((upper == 1) & (major == halves - 1))
         def _():
-            finish(1, slots, 2)
+            finish((1,), slots, 2)
 
         return carry
 

time: 27 us -> 26.8 us (level)
  no operation moved by 1% of the time
where the time goes in v8:
time: 26.8 us; the launch traced here: 26.4 us
  Pallas kernels  26.4 us (99%)
    pallas_call x1, Pallas kernels, body(): pl.pallas_call(functools.partial(kernel, parts, heads), out_shape=[jax.Sh...  23.9 us
    pallas_call x1, Pallas kernels, body(): pl.pallas_call(final_kernel, out_shape=jax.ShapeDtypeStruct((rows, width)...  2.52 us

profile of v8, /device:TPU:18, one launch (start us, length us, event | category | flops | bytes accessed | tf_op | source)
XLA Modules:
  0.0 26.4 jit_solution(2603215613941042898)
XLA Ops:
  0.0 23.9 %shard_map.73 = (bf16[8,96,128]{2,1,0:T(8,128)(2,1)}, bf16[4,96,128]{2,1,0:T(8,128)(2,1)}, bf16[192,512]{1,0:T(8,128)(2,1)}) custom-call(bf16[192,512]{1,0:T(8,128)(2,1)} %tokens_hbm.3, s32[1,192]{1,0:T(1,128)} %bitcast.5, f32[1,512]{1,0:T(1,128)} %bitcast.3, bf16[512,2048]{1,0:T(8,128)(2,1)} %w_proj_hbm.1, f32[8,16]{1,0:T(8,128)} %bias_hbm.1), custom_call_target="tpu_custom_call" | custom-call | tf_op jit(solution)/shard_map/pallas_call | solution.py:782
  23.9 2.5 %shard_map.74 = bf16[192,512]{1,0:T(8,128)(2,1)} custom-call(bf16[8,96,128]{2,1,0:T(8,128)(2,1)} %get-tuple-element.8.att_hbm, bf16[4,96,128]{2,1,0:T(8,128)(2,1)} %get-tuple-element.9.part_hbm, bf16[192,512]{1,0:T(8,128)(2,1)} %get-tuple-element.10.gate_hbm, bf16[192,512]{1,0:T(8,128)(2,1)} %tokens_hbm.3, f32[1,512]{1,0:T(1,128)} %bitcast.4, ...), custom_call_target="tpu_custom_call" | custom-call | tf_op jit(solution)/shard_map/pallas_call | solution.py:836
